TPU v7x, 128 devices: a whole 4x4x4 slice. The times are simulated.
128 devices in a mesh: lon: 8 (over y, core), lat: 16 (over x, z).
Axes of the slice: x: 4, y: 4, z: 4, core: 2. Of those that a mesh axis runs over, the one named last changes fastest.
Arguments:
- state_pert: bfloat16 [64, 32, 6, 128, 256], P('lon', 'lat'), may hold values from -6 to 6
- state_mean: float32 [64, 32, 6, 256], P('lon', 'lat'), may hold values from -6 to 6
- obs_anom: bfloat16 [24576, 128, 128], P(('lon', 'lat')), may hold values from -6 to 6
- innov: float32 [24576, 128], P(('lon', 'lat')), may hold values from -12 to 12
- obs_rinv: float32 [24576, 128], P(('lon', 'lat')), may hold values from 0.25 to 4
- obs_lon: int32 [24576, 128], P(('lon', 'lat')), may hold values from 0 to 1023, as said below
- obs_lat: int32 [24576, 128], P(('lon', 'lat')), may hold values from 40 to 471, as said below
- block_list: int32 [64, 32, 48], P('lon', 'lat'), may hold values from 0 to 24575, as said below
- block_count: int32 [64, 32], P('lon', 'lat'), may hold values from 6 to 48
Outputs:
- analysis: float32 [64, 32, 6, 128, 256], P('lon', 'lat')
Inputs may be any that keep to these rules, and one draw needn't show every extreme that they name: `block_list`: block b is held by the device of flat index b // 192 over lon+lat. The first 48 entries of a patch's list name distinct blocks. Over all list entries of the patches of one device, each holder holds exactly 6 of the named blocks (counting repeats over patches). Only the first block_count entries of a patch's list are used. `obs_lon`: the longitude indices of one block's observations lie within 32 consecutive columns, counted around the periodic grid. `obs_lat`: the latitude indices of one block's observations lie within 32 consecutive columns.
All inputs are finite; a program needn't handle non-finite values.
Results may differ from a plain program's by a relative error of at most 0.0023.
Values may be sent and summed in bfloat16 or wider, within the bound.
A program may use at most 192 MiB of HBM per device.

v0:
```python
import functools

import jax
import jax.numpy as jnp
from jax import lax
from jax.sharding import Mesh
from jax.sharding import PartitionSpec as P

PSIDE = 16
NS_ITERS = 5
LON_LAT = ("lon_0", "lon_1", "lat_0", "lat_1")
LON = ("lon_0", "lon_1")
LAT = ("lat_0", "lat_1")


loc_scale = 48.0


def by_axis(shard, axes):
    return functools.reduce(lax.psum, axes, shard)


def in_blocks(shard, dim, length):
    before, after = (shard.shape[:dim], shard.shape[dim + 1 :])
    return jnp.moveaxis(shard.reshape(*before, length, -1, *after), dim, 0)


def edges_of(length, count):
    turn = length // count
    if turn >= 8:
        turn -= turn % 8
    return [turn * k for k in range(1, count)]


def in_order(parts, dim):
    lengths = list(parts.shape[1:])
    lengths[dim] *= parts.shape[0]
    return jnp.moveaxis(parts, 0, dim).reshape(lengths)


def cut_exchange(shard, axis, pieces, split_dim, concat_dim):
    parts = in_blocks(shard, split_dim, lax.axis_size(axis))
    widest = max(range(1, max(2, parts.ndim - 1)), key=lambda d: parts.shape[d])
    finished = []
    for piece in jnp.split(parts, edges_of(parts.shape[widest], pieces), axis=widest):
        if piece.size:
            finished.append(lax.all_to_all(piece, axis, split_axis=0, concat_axis=0, tiled=True))
    return in_order(jnp.concatenate(finished, axis=widest), concat_dim)


def product(left, right):
    return jnp.dot(left, right, precision=lax.Precision.HIGHEST)


def analyse(
    deviations,
    centre_state,
    anomalies,
    obs_fields,
    used_count,
    centre_lon,
    centre_lat,
    inflation,
    grid_lon,
):
    members = anomalies.shape[1]
    in_list = (jnp.arange(anomalies.shape[0]) < used_count).astype(jnp.float32)
    lon_gap = jnp.abs(obs_fields[:, 2] - centre_lon)
    lon_gap = jnp.minimum(lon_gap, grid_lon - lon_gap)
    lat_gap = obs_fields[:, 3] - centre_lat
    weight = (
        obs_fields[:, 1]
        * jnp.exp(-(lon_gap * lon_gap + lat_gap * lat_gap) / (2.0 * loc_scale * loc_scale))
        * in_list[:, None]
    )
    scaled = (anomalies * weight[:, None, :]).astype(jnp.bfloat16)
    gram_matrix = jnp.einsum("lko,lmo->km", scaled, anomalies, preferred_element_type=jnp.float32)
    projected = jnp.einsum(
        "lko,lo->k", scaled.astype(jnp.float32), obs_fields[:, 0], precision=lax.Precision.HIGHEST
    )
    identity = jnp.eye(members, dtype=jnp.float32)
    system = (members - 1) / inflation * identity + gram_matrix
    scaling = jnp.sqrt(jnp.sum(system * system))
    root = system / scaling
    inverse_root = identity
    for _ in range(NS_ITERS):
        factor = 1.5 * identity - 0.5 * product(inverse_root, root)
        root = product(root, factor)
        inverse_root = product(factor, inverse_root)
    inverse_sqrt = inverse_root / jnp.sqrt(scaling)
    mean_weights = product(inverse_sqrt, product(inverse_sqrt, projected[:, None]))
    weights = (jnp.sqrt(jnp.float32(members - 1)) * inverse_sqrt + mean_weights).astype(
        jnp.bfloat16
    )
    change = jnp.einsum("fjc,jk->fkc", deviations, weights, preferred_element_type=jnp.float32)
    return centre_state[:, None, :] + change


def on_device(
    state_pert, state_mean, obs_anom, innov, obs_rinv, obs_lon, obs_lat, block_list, block_count
):
    holders = lax.axis_size(LON_LAT)
    lon_devices = lax.axis_size(LON)
    lon_patches, lat_patches, fields, members, columns = state_pert.shape
    list_length = block_list.shape[2]
    held_blocks, _, block_obs = obs_anom.shape
    slot_total = lon_patches * lat_patches * list_length
    per_owner = slot_total // holders
    spread = jnp.einsum("bko,bko->bo", obs_anom, obs_anom, preferred_element_type=jnp.float32) / (
        members - 1
    )
    totals = (
        by_axis(jnp.sum(obs_rinv * innov * innov), LON_LAT),
        by_axis(jnp.sum(obs_rinv * spread), LON_LAT),
    )
    total_obs = holders * held_blocks * block_obs
    inflation = totals[0] / (totals[1] + total_obs)
    wanted = block_list.reshape(slot_total)
    holder = wanted // held_blocks
    held_index = wanted % held_blocks
    slot_order = jnp.arange(slot_total)
    earlier_same = (holder[:, None] == holder[None, :]) & (
        slot_order[None, :] < slot_order[:, None]
    )
    slot_rank = jnp.sum(earlier_same.astype(jnp.int32), axis=1)
    bucket = holder * per_owner + slot_rank
    requests = jnp.zeros((holders * per_owner,), jnp.int32).at[bucket].set(held_index)
    obs_fields = jnp.stack(
        [innov, obs_rinv, obs_lon.astype(jnp.float32), obs_lat.astype(jnp.float32)], axis=1
    )
    asked_for = lax.all_to_all(
        requests.reshape(holders, per_owner), LON_LAT, split_axis=0, concat_axis=0, tiled=True
    )
    got_anomalies = cut_exchange(obs_anom[asked_for], LON_LAT, 2, 0, 0)
    got_fields = lax.all_to_all(
        obs_fields[asked_for], LON_LAT, split_axis=0, concat_axis=0, tiled=True
    )
    patch_total = lon_patches * lat_patches
    slot_anomalies = got_anomalies.reshape(holders * per_owner, members, block_obs)[bucket]
    slot_anomalies = slot_anomalies.reshape(patch_total, list_length, members, block_obs)
    slot_fields = got_fields.reshape(holders * per_owner, 4, block_obs)[bucket]
    slot_fields = slot_fields.reshape(patch_total, list_length, 4, block_obs)
    patch_index = jnp.arange(patch_total)
    lon_first = lax.axis_index(LON) * lon_patches
    lat_first = lax.axis_index(LAT) * lat_patches
    centre_lon = ((lon_first + patch_index // lat_patches) * PSIDE).astype(jnp.float32) + (
        PSIDE - 1
    ) / 2.0
    centre_lat = ((lat_first + patch_index % lat_patches) * PSIDE).astype(jnp.float32) + (
        PSIDE - 1
    ) / 2.0
    grid_lon = jnp.float32(lon_devices * lon_patches * PSIDE)

    def patch_update(inputs):
        deviations, centre_state, anomalies, fields_here, used_count, lon_centre, lat_centre = (
            inputs
        )
        return analyse(
            deviations,
            centre_state,
            anomalies,
            fields_here,
            used_count,
            lon_centre,
            lat_centre,
            inflation,
            grid_lon,
        )

    inputs = (
        state_pert.reshape(patch_total, fields, members, columns),
        state_mean.reshape(patch_total, fields, columns),
        slot_anomalies,
        slot_fields,
        block_count.reshape(patch_total),
        centre_lon,
        centre_lat,
    )
    updated = lax.map(patch_update, inputs)
    return updated.reshape(lon_patches, lat_patches, fields, members, columns)


def solution(mesh):
    split = Mesh(mesh.devices.reshape(4, 2, 4, 4), ("lon_0", "lon_1", "lat_0", "lat_1"))
    in_specs = (
        P(LON, LAT, None, None, None),
        P(LON, LAT, None, None),
        P(LON_LAT, None, None),
        P(LON_LAT, None),
        P(LON_LAT, None),
        P(LON_LAT, None),
        P(LON_LAT, None),
        P(LON, LAT, None),
        P(LON, LAT),
    )
    out_specs = P(LON, LAT, None, None, None)
    return jax.shard_map(
        on_device, mesh=split, in_specs=in_specs, out_specs=out_specs, check_vma=False
    )
```

profile of v0, /device:TPU:1, one launch (start us, length us, event | category | flops | bytes accessed | tf_op | source)
XLA Modules:
  0.0 728.4 jit_solution(5975563733071711157)
XLA Ops:
  2.3 3.4 scatter_custom_fusion
  6.4 11.5 %all-to-all-start = ((s32[128,1,6]{2,1,0:T(1,128)}), s32[128,1,6]{2,1,0:T(1,128)S(1)}, u32[]{:S(2)}, u32[]{:S(2)}) async-start(s32[128,1,6]{2,1,0:T(1,128)} %bitcast.24), calls=%async_computation | async-start | bytes 131072 | tf_op jit(solution)/shard_map/all_to_all | solution.py:131
  21.1 6.4 all-to-all-done
  27.6 3.4 gather_fusion.2
  31.0 4.5 all-to-all-start.3
  35.5 22.0 %gather_fusion = bf16[768,128,128]{2,1,0:T(8,128)(2,1)} fusion(bf16[192,128,128]{2,1,0:T(8,128)(2,1)} %param.13, s32[1024]{0:T(1024)S(1)} %pad_clamp_fusion.1), kind=kCustom, calls=%fused_computation | custom fusion | bytes 50334720 | tf_op jit(solution)/shard_map/gather | solution.py:134
  57.5 22.0 %fusion.67 = (bf16[128,1,6,64,128]{4,3,2,1,0:T(8,128)(2,1)}, bf16[128,1,6,64,128]{4,3,2,1,0:T(8,128)(2,1)}) fusion(bf16[128,1,6,128,128]{4,3,2,1,0:T(8,128)(2,1)} %bitcast.197), kind=kLoop, calls=%fused_computation.104 | loop fusion | bytes 50331648 | tf_op jit(solution)/shard_map/split | solution.py:45
  79.5 152.5 %all_to_all.27 = bf16[128,1,6,64,128]{4,3,2,1,0:T(8,128)(2,1)} all-to-all(bf16[128,1,6,64,128]{4,3,2,1,0:T(8,128)(2,1)} %get-tuple-element.188), channel_id=1, replica_groups=mesh['lon_0'=4,'lon_1'=2,'lat_0'=4,'lat_1'=4] {'lon_0','lon_1','lat_0','..., dimensions={0} | all-to-all | bytes 25165824 | tf_op jit(solution)/shard_map/all_to_all | solution.py:47
  232.1 5.1 all-to-all-start.2
  237.1 5.2 fusion.50
  243.0 155.1 %all-reduce.2 = (f32[]{:T(128)}, f32[]{:T(128)}) all-reduce(f32[]{:T(128)} %get-tuple-element.153, f32[]{:T(128)} %get-tuple-element.152), channel_id=1, replica_groups=mesh['lon_0'=4,'lon_1'=2,'lat_0'=4,'lat_1'=4] {'lon_0'}, use_global_device_ids=true, to_apply=%region_3.0 | all-reduce | flops 2 | bytes 16 | tf_op jit(solution)/shard_map/psum | solution.py:20
  398.1 4.1 all-reduce.3
  402.2 6.7 all-reduce.1
  409.0 11.3 %all-reduce = (f32[]{:T(128)}, f32[]{:T(128)}) all-reduce(f32[]{:T(128)} %get-tuple-element.176, f32[]{:T(128)} %get-tuple-element.177), channel_id=1, replica_groups=mesh['lon_0'=4,'lon_1'=2,'lat_0'=4,'lat_1'=4] {'lat_1'}, use_global_device_ids=true, to_apply=%region_6.0 | all-reduce | flops 2 | bytes 16 | tf_op jit(solution)/shard_map/psum | solution.py:20
  424.5 22.3 %pad_maximum_fusion = bf16[128,1,6,128,128]{4,3,2,1,0:T(8,128)(2,1)} fusion(bf16[128,1,6,64,128]{4,3,2,1,0:T(8,128)(2,1)} %all-to-all-done.2, bf16[128,1,6,64,128]{4,3,2,1,0:T(8,128)(2,1)} %all_to_all.27), kind=kLoop, calls=%fused_computation.63 | loop fusion | flops 50331648 | bytes 50331648 | tf_op jit(solution)/shard_map/concatenate | solution.py:48
  446.9 27.4 %gather_fusion.1 = bf16[768,128,128]{2,1,0:T(8,128)(2,1)} fusion(bf16[768,128,128]{2,1,0:T(8,128)(2,1)} %bitcast.198, s32[1024]{0:T(1024)S(1)} %pad_clamp_fusion), kind=kCustom, calls=%fused_computation.1 | custom fusion | bytes 50334720 | tf_op jit(solution)/shard_map/gather | solution.py:139
  474.2 254.2 %while.12 = (s32[]{:T(128)}, f32[16,6,128,256]{3,2,1,0:T(8,128)}, f32[16,6,256]{2,1,0:T(8,128)S(1)}, f32[]{:T(128)}, bf16[16,48,128,128]{3,2,1,0:T(8,128)(2,1)},...) while((s32[]{:T(128)}, f32[16,6,128,256]{3,2,1,0:T(8,128)}, ...), condition=%wide.region_14.15_spmd, body=%wide.region_12.14_spmd.sunk | while | flops 619339904 | bytes 9421381 | solution.py:179
  477.9 3.1 multiply_reduce_fusion.3
  493.8 3.1 multiply_reduce_fusion.3
  509.7 3.1 multiply_reduce_fusion.3
  525.5 3.2 multiply_reduce_fusion.3
  541.4 3.2 multiply_reduce_fusion.3
  557.4 3.2 multiply_reduce_fusion.3
  573.3 3.1 multiply_reduce_fusion.3
  589.2 3.1 multiply_reduce_fusion.3
  605.0 3.1 multiply_reduce_fusion.3
  620.9 3.1 multiply_reduce_fusion.3
  636.7 3.1 multiply_reduce_fusion.3
  652.6 3.1 multiply_reduce_fusion.3
  668.5 3.2 multiply_reduce_fusion.3
  684.4 3.2 multiply_reduce_fusion.3
  700.3 3.1 multiply_reduce_fusion.3
  (452 shorter events, 203.6 us)
Async XLA Ops:
  6.4 21.0 %all-to-all-start = ((s32[128,1,6]{2,1,0:T(1,128)}), s32[128,1,6]{2,1,0:T(1,128)S(1)}, u32[]{:S(2)}, u32[]{:S(2)}) async-start(s32[128,1,6]{2,1,0:T(1,128)} %bitcast.24), calls=%async_computation | async-start | bytes 131072 | tf_op jit(solution)/shard_map/all_to_all | solution.py:131
  31.0 48.5 %all-to-all-start.3 = ((f32[128,6,4,128]{3,2,1,0:T(4,128)}), f32[128,6,4,128]{3,2,1,0:T(4,128)S(1)}, u32[]{:S(2)}, u32[]{:S(2)}) async-start(f32[128,6,4,128]{3,2,1,0:T(4,128)} %bitcast.33), calls=%async_computation.3 | async-start | bytes 3145728 | tf_op jit(solution)/shard_map/all_to_all | solution.py:135
  232.1 10.3 %copy-start = (f32[192,128]{1,0:T(8,128)S(1)}, f32[192,128]{1,0:T(8,128)}, u32[]{:S(2)}) copy-start(f32[192,128]{1,0:T(8,128)} %param.14) | copy-start | bytes 294916
  232.1 10.3 %copy-start.1 = (f32[192,128]{1,0:T(8,128)S(1)}, f32[192,128]{1,0:T(8,128)}, u32[]{:S(2)}) copy-start(f32[192,128]{1,0:T(8,128)} %param.15) | copy-start | bytes 294916
  232.1 188.2 %copy-start.2 = (f32[8,2,6,256]{3,1,2,0:T(2,128)S(1)}, f32[8,2,6,256]{3,1,2,0:T(2,128)}, u32[]{:S(2)}) copy-start(f32[8,2,6,256]{3,1,2,0:T(2,128)} %param.12) | copy-start | bytes 294916
  232.1 188.2 %copy-start.3 = (s32[8,2]{0,1:T(2,128)S(1)}, s32[8,2]{0,1:T(2,128)}, u32[]{:S(2)}) copy-start(s32[8,2]{0,1:T(2,128)} %param.19) | copy-start | bytes 196
  232.1 192.5 %all-to-all-start.2 = ((bf16[128,1,6,64,128]{4,3,2,1,0:T(8,128)(2,1)}), bf16[128,1,6,64,128]{4,3,2,1,0:T(8,128)(2,1)}, u32[]{:S(2)}, u32[]{:S(2)}) async-start(bf16[128,1,6,64,128]{4,3,2,1,0:T(8,128)(2,1)} %get-tuple-element.189), calls=%async_computation.2 | async-start | bytes 25165824 | tf_op jit(solution)/shard_map/all_to_all | solution.py:47
where the time goes:
time: 734 us; the launch traced here: 728 us
  blocking collectives  330 us (45%)
  matrix products  182 us (25%)
  local copies, waits for them, and re-layouts  111 us (15%)
  other arithmetic  63.2 us (9%)
  starting transfers between devices  21.1 us (3%)
  loops' own time  13.6 us (2%)
    psum x4, blocking collectives, by_axis(): return functools.reduce(lax.psum, axes, shard)  177 us
    all_to_all x1, blocking collectives, cut_exchange(): lax.all_to_all(piece, axis, split_axis=0, concat_axis=0, tiled=True)  153 us
    dot_general x256, matrix products, product(): return jnp.dot(left, right, precision=lax.Precision.HIGHEST)  51.7 us
    dot_general x16, matrix products, analyse(): jnp.einsum('lko,lmo->km', scaled, anomalies, preferred_element_type=jnp.f...  49.9 us
    dot_general x16, matrix products, analyse(): jnp.einsum('lko,lo->k', scaled.astype(jnp.float32), obs_fields[:, 0], pre...  43.7 us
    dot_general x16, matrix products, analyse(): jnp.einsum('fjc,jk->fkc', deviations, weights, preferred_element_type=jnp...  36.5 us
    dynamic_slice x80, local copies, waits for them, and re-layouts, on_device(): updated = lax.map(patch_update, inputs)  28.6 us
    gather x1, local copies, waits for them, and re-layouts, on_device(): got_anomalies.reshape(holders * per_owner, members, block_obs)[bucket]  27.4 us
  transfers between devices with their start and end apart: 3, of which 1 were waited for; matrix products, arithmetic and copies ran while one was open for 8% of the time, Pallas kernels for 0%

commit v1 on v0

v1 whole, which is shorter than its diff:
```python
import functools

import jax
import jax.numpy as jnp
from jax import lax
from jax.experimental import pallas as pl
from jax.experimental.pallas import tpu as pltpu
from jax.sharding import PartitionSpec as P

PSIDE = 16
NS_ITERS = 5
LOC_SCALE = 48.0
AXES = ("lon", "lat")
F32 = jnp.float32
BF16 = jnp.bfloat16


def totals_kernel(anom_ref, rinv_ref, innov_ref, out_ref, ext_ref):
    step = pl.program_id(0)
    blocks = anom_ref.shape[0]

    @pl.when(step == 0)
    def _():
        out_ref[...] = jnp.zeros_like(out_ref)

    innov = innov_ref[...]
    rinv = rinv_ref[...]
    high = innov.astype(BF16)
    rest = innov - high.astype(F32)
    mid = rest.astype(BF16)
    low = (rest - mid.astype(F32)).astype(BF16)
    ext = jnp.concatenate(
        [high[:, None, :].astype(F32), mid[:, None, :].astype(F32), low[:, None, :].astype(F32)]
        + [jnp.zeros((blocks, 13, innov.shape[1]), F32)],
        axis=1,
    )
    ext_ref[...] = ext.astype(BF16)
    out_ref[0:8, :] += jnp.sum((rinv * innov * innov).reshape(blocks // 8, 8, -1), axis=0)

    total = jnp.zeros((8, innov.shape[1]), F32)
    for b in range(blocks):
        a = anom_ref[b].astype(F32)
        squares = jnp.sum((a * a).reshape(-1, 8, a.shape[1]), axis=0)
        total = total + squares * rinv[b : b + 1, :]
    out_ref[8:16, :] += total


def gram_kernel(per, lat_devices, lon_patches, lat_patches, code_ref, anom_ref, ext_ref, rinv_ref,
                lon_ref, lat_ref, out_ref):
    count = out_ref.shape[0]
    first = pl.program_id(0) * count
    members = anom_ref.shape[1]
    half = members // 2
    grid_lon = float(8 * lon_patches * PSIDE)
    row = lax.broadcasted_iota(jnp.int32, (half, members), 0)
    lane = lax.broadcasted_iota(jnp.int32, (half, members), 1)
    keep = (lane >= half) | (row >= lane)
    on_diag = row == lane
    row8 = lax.broadcasted_iota(jnp.int32, (8, members), 0)

    def one(i, carry):
        who = first + i
        diags = jnp.zeros((8, members), F32)
        projs = jnp.zeros((8, members), F32)
        for s in range(per):
            code = code_ref[who * 8 + s]
            valid = code % 2
            patch = (code // 2) % 16
            held = code // 32
            cl = ((who // lat_devices) * lon_patches + patch // lat_patches) * PSIDE
            ct = ((who % lat_devices) * lat_patches + patch % lat_patches) * PSIDE
            cl = cl.astype(F32) + (PSIDE - 1) / 2.0
            ct = ct.astype(F32) + (PSIDE - 1) / 2.0
            gap = jnp.abs(lon_ref[pl.ds(held, 1), :] - cl)
            gap = jnp.minimum(gap, grid_lon - gap)
            other = lat_ref[pl.ds(held, 1), :] - ct
            weight = rinv_ref[pl.ds(held, 1), :] * jnp.exp(
                -(gap * gap + other * other) / (2.0 * LOC_SCALE * LOC_SCALE)
            )
            weight = weight * valid.astype(F32)
            a = anom_ref[held]
            scaled = (a.astype(F32) * weight).astype(BF16)
            left = jnp.concatenate([a, ext_ref[held]], axis=0)
            full = lax.dot_general(
                left, scaled, (((1,), (1,)), ((), ())), preferred_element_type=F32
            )
            top = full[:half, :]
            low = pltpu.roll(full[half:members, :], half, 1)
            out_ref[i, s * half : (s + 1) * half, :] = jnp.where(keep, top, low).astype(BF16)
            diag = jnp.sum(jnp.where(on_diag, low, 0.0), axis=0, keepdims=True)
            proj = jnp.sum(full[members : members + 8, :], axis=0, keepdims=True)
            diags = jnp.where(row8 == s, diag, diags)
            projs = jnp.where(row8 == s, proj, projs)
        high = projs.astype(BF16).astype(F32)
        extra = jnp.concatenate([diags, high, projs - high, jnp.zeros_like(high)], axis=0)
        out_ref[i, per * half : per * half + 32, :] = extra.astype(BF16)
        return carry

    lax.fori_loop(0, count, one, 0)


def gather_kernel(per, patch_ref, got_ref, acc_ref):
    count = got_ref.shape[0]
    step = pl.program_id(0)
    half = (got_ref.shape[1] - 32) // per

    @pl.when(step == 0)
    def _():
        acc_ref[...] = jnp.zeros_like(acc_ref)

    def one(i, carry):
        extra = got_ref[i, per * half :, :].astype(F32)
        proj = extra[8:16, :] + extra[16:24, :]
        for s in range(per):
            patch = patch_ref[(step * count + i) * per + s]
            acc_ref[patch, 0:half, :] += got_ref[i, s * half : (s + 1) * half, :].astype(F32)
            pair = jnp.concatenate(
                [extra[s : s + 1, :], proj[s : s + 1, :], jnp.zeros((6, proj.shape[1]), F32)], axis=0
            )
            acc_ref[patch, half : half + 8, :] += pair
        return carry

    lax.fori_loop(0, count, one, 0)


def halves(x):
    high = x.astype(BF16)
    return high, (x - high.astype(F32)).astype(BF16)


def product(left, right):
    n = right[0].shape[1]
    lhs = jnp.concatenate([left[0], left[1]], axis=1)
    upper = jnp.concatenate([right[0], right[1]], axis=1)
    lower = jnp.concatenate([right[0], jnp.zeros_like(right[1])], axis=1)
    both = jnp.dot(lhs, jnp.concatenate([upper, lower], axis=0), preferred_element_type=F32)
    return both[:, :n] + both[:, n:]


def update_kernel(base_ref, acc_ref, pert_ref, mean_ref, out_ref):
    count, fields, members, _ = pert_ref.shape
    half = members // 2
    row = lax.broadcasted_iota(jnp.int32, (members, members), 0)
    lane = lax.broadcasted_iota(jnp.int32, (members, members), 1)
    eye = jnp.where(row == lane, 1.0, 0.0)
    r = row[:half]
    c = lane[:half]
    base = base_ref[0]
    state = []
    for q in range(count):
        packed = acc_ref[q, 0:half, :]
        top = jnp.where((c >= half) | (r > c), packed, 0.0)
        low = pltpu.roll(jnp.where((c < half) & (r < c), packed, 0.0), half, 1)
        part = jnp.concatenate([top, low], axis=0)
        own = jnp.sum(jnp.where(r == c, packed, 0.0), axis=0, keepdims=True)
        own = own + pltpu.roll(acc_ref[q, half : half + 1, :], half, 1)
        system = part + part.T + jnp.where(row == lane, own + base, 0.0)
        scaling = jnp.sqrt(jnp.sum(jnp.sum(system * system, axis=0, keepdims=True), axis=1, keepdims=True))
        root = system / scaling
        factor = 1.5 * eye - 0.5 * root
        state.append([product(halves(root), halves(factor)), factor, scaling])
    for it in range(1, NS_ITERS):
        for q in range(count):
            root, inverse, _ = state[q]
            inverse2 = halves(inverse)
            factor = 1.5 * eye - 0.5 * product(inverse2, halves(root))
            factor2 = halves(factor)
            state[q][1] = product(factor2, inverse2)
            if it < NS_ITERS - 1:
                state[q][0] = product(factor2, halves(root))
    for q in range(count):
        _, inverse, scaling = state[q]
        inverse = inverse * (1.0 / jnp.sqrt(scaling))
        proj = acc_ref[q, half + 1 : half + 2, :]
        inverse2 = halves(inverse)
        mean = jnp.broadcast_to(proj, (8, members))
        mean = product(halves(mean), inverse2)
        mean = product(halves(mean), inverse2)[0:1, :]
        weights = (float(members - 1) ** 0.5 * inverse + mean).astype(BF16)
        for f in range(fields):
            change = jnp.dot(weights, pert_ref[q, f], preferred_element_type=F32)
            out_ref[q, f] = mean_ref[q, f : f + 1, :] + change


def on_device(
    state_pert, state_mean, obs_anom, innov, obs_rinv, obs_lon, obs_lat, block_list, block_count
):
    holders = lax.axis_size(AXES)
    lat_devices = lax.axis_size("lat")
    lon_patches, lat_patches, fields, members, columns = state_pert.shape
    patches = lon_patches * lat_patches
    list_length = block_list.shape[2]
    held_blocks, _, block_obs = obs_anom.shape
    slots = patches * list_length
    per = slots // holders
    half = members // 2
    rows = per * half + 32

    step_blocks = 16
    sums, ext = pl.pallas_call(
        totals_kernel,
        grid=(held_blocks // step_blocks,),
        in_specs=[
            pl.BlockSpec((step_blocks, members, block_obs), lambda i: (i, 0, 0)),
            pl.BlockSpec((step_blocks, block_obs), lambda i: (i, 0)),
            pl.BlockSpec((step_blocks, block_obs), lambda i: (i, 0)),
        ],
        out_specs=[
            pl.BlockSpec((16, block_obs), lambda i: (0, 0)),
            pl.BlockSpec((step_blocks, 16, block_obs), lambda i: (i, 0, 0)),
        ],
        out_shape=[
            jax.ShapeDtypeStruct((16, block_obs), F32),
            jax.ShapeDtypeStruct((held_blocks, 16, block_obs), BF16),
        ],
        name="totals",
    )(obs_anom, obs_rinv, innov)
    first_sum = jnp.sum(sums[0:8])
    second_sum = jnp.sum(sums[8:16]) / (members - 1)

    wanted = block_list.reshape(slots)
    holder = wanted // held_blocks
    slot = jnp.arange(slots)
    patch = slot // list_length
    valid = (slot % list_length < jnp.repeat(block_count.reshape(patches), list_length)).astype(jnp.int32)
    code = ((wanted % held_blocks) * 16 + patch) * 2 + valid
    earlier = (holder[:, None] == holder[None, :]) & (slot[None, :] < slot[:, None])
    rank = jnp.sum(earlier.astype(jnp.int32), axis=1)
    bucket = holder * per + rank
    requests = jnp.sum(jnp.where(bucket[:, None] == slot[None, :], code[:, None], 0), axis=0)
    message = jnp.concatenate(
        [
            requests.reshape(holders, per).astype(F32),
            jnp.broadcast_to(jnp.stack([first_sum, second_sum])[None, :], (holders, 2)),
        ],
        axis=1,
    )
    asked = lax.all_to_all(message, AXES, split_axis=0, concat_axis=0, tiled=True)
    total = jnp.sum(asked[:, per:], axis=0)
    inflation = total[0] / (total[1] + holders * held_blocks * block_obs)
    base = ((members - 1) / inflation).reshape(1)
    codes = asked.astype(jnp.int32).reshape(holders * 8)

    turn = 8
    whole3 = lambda i: (0, 0, 0)
    whole2 = lambda i: (0, 0)
    grams = pl.pallas_call(
        functools.partial(gram_kernel, per, lat_devices, lon_patches, lat_patches),
        grid=(holders // turn,),
        in_specs=[
            pl.BlockSpec(memory_space=pltpu.SMEM),
            pl.BlockSpec((held_blocks, members, block_obs), whole3),
            pl.BlockSpec((held_blocks, 16, block_obs), whole3),
            pl.BlockSpec((held_blocks, block_obs), whole2),
            pl.BlockSpec((held_blocks, block_obs), whole2),
            pl.BlockSpec((held_blocks, block_obs), whole2),
        ],
        out_specs=pl.BlockSpec((turn, rows, members), lambda i: (i, 0, 0)),
        out_shape=jax.ShapeDtypeStruct((holders, rows, members), BF16),
        name="grams",
    )(codes, obs_anom, ext, obs_rinv, obs_lon.astype(F32), obs_lat.astype(F32))

    got = lax.all_to_all(grams, AXES, split_axis=0, concat_axis=0, tiled=True)

    patch_of = (requests // 2) % 16
    acc = pl.pallas_call(
        functools.partial(gather_kernel, per),
        grid=(holders // turn,),
        in_specs=[
            pl.BlockSpec(memory_space=pltpu.SMEM),
            pl.BlockSpec((turn, rows, members), lambda i: (i, 0, 0)),
        ],
        out_specs=pl.BlockSpec((patches, half + 8, members), whole3),
        out_shape=jax.ShapeDtypeStruct((patches, half + 8, members), F32),
        name="gather",
    )(patch_of, got)

    pair = 2
    updated = pl.pallas_call(
        update_kernel,
        grid=(patches // pair,),
        in_specs=[
            pl.BlockSpec(memory_space=pltpu.SMEM),
            pl.BlockSpec((pair, half + 8, members), lambda i: (i, 0, 0)),
            pl.BlockSpec((pair, fields, members, columns), lambda i: (i, 0, 0, 0)),
            pl.BlockSpec((pair, fields, columns), lambda i: (i, 0, 0)),
        ],
        out_specs=pl.BlockSpec((pair, fields, members, columns), lambda i: (i, 0, 0, 0)),
        out_shape=jax.ShapeDtypeStruct((patches, fields, members, columns), F32),
        name="update",
    )(
        base,
        acc,
        state_pert.reshape(patches, fields, members, columns),
        state_mean.reshape(patches, fields, columns),
    )
    return updated.reshape(lon_patches, lat_patches, fields, members, columns)


def solution(mesh):
    in_specs = (
        P("lon", "lat", None, None, None),
        P("lon", "lat", None, None),
        P(AXES, None, None),
        P(AXES, None),
        P(AXES, None),
        P(AXES, None),
        P(AXES, None),
        P("lon", "lat", None),
        P("lon", "lat"),
    )
    out_specs = P("lon", "lat", None, None, None)
    return jax.shard_map(
        on_device, mesh=mesh, in_specs=in_specs, out_specs=out_specs, check_vma=False
    )
```

time: 734 us -> 324 us (0.44)
  blocking collectives: 330 us -> 0 us
  waiting for transfers between devices: 6.37 us -> 190 us
  matrix products: 182 us -> 0 us
  local copies, waits for them, and re-layouts: 111 us -> 3.41 us
  Pallas kernels: 0 us -> 104 us
  other arithmetic: 63.2 us -> 6.86 us
  loops' own time: 13.6 us -> 0 us
    all_to_all x3 -> x2, waiting for transfers between devices: 6.37 us -> 190 us  [the longest x1 182 us: on_device(): got = lax.all_to_all(grams, AXES, split_axis=0, concat_axis=0, tiled=True)]
    dot_general x304 -> x0, matrix products: 182 us -> none  [the longest x256 51.7 us: product(): return jnp.dot(left, right, precision=lax.Precision.HIGHEST)]
    psum x4 -> x0, blocking collectives: 177 us -> none  [by_axis(): return functools.reduce(lax.psum, axes, shard)]
    all_to_all x1 -> x0, blocking collectives: 153 us -> none  [cut_exchange(): lax.all_to_all(piece, axis, split_axis=0, concat_axis=0, tiled=True)]
    pallas_call x0 -> x4, Pallas kernels: none -> 104 us  [the longest x1 58.1 us: on_device(): pl.pallas_call(functools.partial(gram_kernel, per, lat_devices, lon_patch...]
    gather x4 -> x0, local copies, waits for them, and re-layouts: 55.6 us -> none  [the longest x1 27.4 us: on_device(): got_anomalies.reshape(holders * per_owner, members, block_obs)[bucket]]
    dynamic_slice x80 -> x0, local copies, waits for them, and re-layouts: 28.6 us -> none  [on_device(): updated = lax.map(patch_update, inputs)]
    split x1 -> x0, local copies, waits for them, and re-layouts: 22 us -> none  [cut_exchange(): jnp.split(parts, edges_of(parts.shape[widest], pieces), axis=widest)]
  transfers between devices with their start and end apart: 3 -> 2, of which waited for: 1 -> 2; matrix products, arithmetic and copies ran while one was open for 8% -> 1% of each run, Pallas kernels for 0% -> 0%
where the time goes in v1:
time: 324 us
  waiting for transfers between devices  190 us (59%)
  Pallas kernels  104 us (32%)
  starting transfers between devices  17.3 us (5%)
  other arithmetic  6.86 us (2%)
  local copies, waits for them, and re-layouts  3.41 us (1%)
    all_to_all x1, waiting for transfers between devices, on_device(): got = lax.all_to_all(grams, AXES, split_axis=0, concat_axis=0, tiled=True)  182 us
    pallas_call x1, Pallas kernels, on_device(): pl.pallas_call(functools.partial(gram_kernel, per, lat_devices, lon_patch...  58.1 us
    pallas_call x1, Pallas kernels, on_device(): pl.pallas_call(update_kernel, grid=(patches // pair,), in_specs=[pl.Block...  23.9 us
    pallas_call x1, Pallas kernels, on_device(): pl.pallas_call(functools.partial(gather_kernel, per), grid=(holders // tu...  13.2 us
    all_to_all x1, starting transfers between devices, on_device(): lax.all_to_all(message, AXES, split_axis=0, concat_axis=0, tiled=True)  11.5 us
    pallas_call x1, Pallas kernels, on_device(): pl.pallas_call(totals_kernel, grid=(held_blocks // step_blocks,), in_spec...  8.73 us
    all_to_all x1, waiting for transfers between devices, on_device(): lax.all_to_all(message, AXES, split_axis=0, concat_axis=0, tiled=True)  8.26 us
  transfers between devices with their start and end apart: 2, of which 2 were waited for; matrix products, arithmetic and copies ran while one was open for 1% of the time, Pallas kernels for 0%

profile of v1, /device:TPU:1, one launch (start us, length us, event | category | flops | bytes accessed | tf_op | source)
XLA Modules:
  0.0 323.6 jit_solution(7450455774548880654)
XLA Ops:
  0.0 0.7 broadcast_divide_fusion
  0.7 0.7 sign_compare_fusion
  1.4 0.1 div.45
  1.5 0.1 ne.97
  1.6 0.1 rem.78
  1.7 0.8 copy.18
  2.4 0.1 reshape.119
  2.5 0.1 broadcast_in_dim.16
  2.6 0.1 reshape.120
  2.7 0.4 convert_reduce_fusion
  3.1 0.3 select_reduce_fusion
  3.4 0.6 add_select_fusion
  4.0 0.1 convert_element_type.32
  4.1 0.0 copy-start.1
  4.1 8.7 %totals.1 = (f32[16,128]{1,0:T(8,128)}, bf16[192,16,128]{2,1,0:T(8,128)(2,1)}) custom-call(bf16[192,128,128]{2,1,0:T(8,128)(2,1)} %anom_ref.3, f32[192,128]{1,0:T(8,128)} %rinv_ref.3, f32[192,128]{1,0:T(8,128)} %innov_ref.1), custom_call_target="tpu_custom_call" | custom-call | tf_op jit(solution)/shard_map/totals/pallas_call | solution.py:200
  12.9 1.3 slice_reduce_fusion.2
  14.8 0.6 pad_maximum_fusion.1
  15.5 0.6 pad_maximum_fusion
  16.1 11.5 %all-to-all-start = ((f32[128,1,8]{2,1,0:T(1,128)}), f32[128,1,8]{2,1,0:T(1,128)S(1)}, u32[]{:S(2)}, u32[]{:S(2)}) async-start(f32[128,1,8]{2,1,0:T(1,128)} %bitcast.3), calls=%async_computation | async-start | bytes 131072 | tf_op jit(solution)/shard_map/all_to_all | solution.py:238
  27.6 0.6 convert_element_type.35.lon_ref
  28.3 0.6 convert_element_type.36.lat_ref
  28.9 8.3 %all-to-all-done = f32[128,1,8]{2,1,0:T(1,128)S(1)} async-done(((f32[128,1,8]{2,1,0:T(1,128)}), f32[128,1,8]{2,1,0:T(1,128)S(1)}, u32[]{:S(2)}, u32[]{:S(2)}) %all-to-all-start) | async-done | bytes 4128 | tf_op jit(solution)/shard_map/all_to_all | solution.py:238
  37.2 0.2 convert_reduce_fusion.1
  37.3 0.7 convert_element_type.34.code_ref
  38.0 58.1 %grams.1 = bf16[128,416,128]{2,1,0:T(8,128)(2,1)} custom-call(s32[1024]{0:T(1024)} %convert_element_type.34.code_ref, bf16[192,128,128]{2,1,0:T(8,128)(2,1)} %anom_ref.3, bf16[192,16,128]{2,1,0:T(8,128)(2,1)} %get-tuple-element.8.ext_ref, f32[192,128]{1,0:T(8,128)} %rinv_ref.3, f32[192,128]{1,0:T(8,128)} %convert_element_type.35.lon_ref, ...), custom_call_target="tpu_custom_call" | custom-call | tf_op jit(solution)/shard_map/grams/pallas_call | solution.py:247
  96.2 5.8 %all-to-all-start.1 = ((bf16[128,416,128]{2,1,0:T(8,128)(2,1)}), bf16[128,416,128]{2,1,0:T(8,128)(2,1)}, u32[]{:S(2)}, u32[]{:S(2)}) async-start(bf16[128,416,128]{2,1,0:T(8,128)(2,1)} %grams.1), calls=%async_computation.1 | async-start | bytes 27262976 | tf_op jit(solution)/shard_map/all_to_all | solution.py:263
  102.0 0.7 copy.20
  102.7 0.1 slice_reduce_fusion
  102.8 0.7 fusion.16
  104.8 181.6 %all-to-all-done.1.got_ref = bf16[128,416,128]{2,1,0:T(8,128)(2,1)} async-done(((bf16[128,416,128]{2,1,0:T(8,128)(2,1)}), bf16[128,416,128]{2,1,0:T(8,128)(2,1)}, u32[]{:S(2)}, u32[]{:S(2)}) %all-to-all-start.1) | async-done | bytes 13631520 | tf_op jit(solution)/shard_map/all_to_all | solution.py:263
  286.4 13.2 %gather.1.acc_ref = f32[16,72,128]{2,1,0:T(8,128)} custom-call(s32[768]{0:T(1024)} %get-tuple-element.13.patch_ref, bf16[128,416,128]{2,1,0:T(8,128)(2,1)} %all-to-all-done.1.got_ref), custom_call_target="tpu_custom_call" | custom-call | tf_op jit(solution)/shard_map/gather/pallas_call | solution.py:266
  299.6 23.9 %update.1 = f32[16,6,128,256]{3,2,1,0:T(8,128)} custom-call(f32[1]{0:T(128)S(6)} %div.48.base_ref, f32[16,72,128]{2,1,0:T(8,128)} %gather.1.acc_ref, bf16[16,6,128,256]{3,2,1,0:T(8,128)(2,1)} %bitcast.9, f32[16,6,256]{2,1,0:T(8,128)} %bitcast.11), custom_call_target="tpu_custom_call" | custom-call | tf_op jit(solution)/shard_map/update/pallas_call | solution.py:279
  (7 shorter events, 0.0 us)
Async XLA Ops:
  4.1 23.5 %copy-start.1 = (s32[192,128]{1,0:T(8,128)S(1)}, s32[192,128]{1,0:T(8,128)}, u32[]{:S(2)}) copy-start(s32[192,128]{1,0:T(8,128)} %param.14) | copy-start | bytes 294916
  4.1 24.1 %copy-start.2 = (s32[192,128]{1,0:T(8,128)S(1)}, s32[192,128]{1,0:T(8,128)}, u32[]{:S(2)}) copy-start(s32[192,128]{1,0:T(8,128)} %param.15) | copy-start | bytes 294916
  16.1 21.1 %all-to-all-start = ((f32[128,1,8]{2,1,0:T(1,128)}), f32[128,1,8]{2,1,0:T(1,128)S(1)}, u32[]{:S(2)}, u32[]{:S(2)}) async-start(f32[128,1,8]{2,1,0:T(1,128)} %bitcast.3), calls=%async_computation | async-start | bytes 131072 | tf_op jit(solution)/shard_map/all_to_all | solution.py:238
  96.2 5.8 %copy-start = (f32[8,2,6,256]{3,1,2,0:T(2,128)S(1)}, f32[8,2,6,256]{3,1,2,0:T(2,128)}, u32[]{:S(2)}) copy-start(f32[8,2,6,256]{3,1,2,0:T(2,128)} %param.10) | copy-start | bytes 294916
  96.2 190.2 %all-to-all-start.1 = ((bf16[128,416,128]{2,1,0:T(8,128)(2,1)}), bf16[128,416,128]{2,1,0:T(8,128)(2,1)}, u32[]{:S(2)}, u32[]{:S(2)}) async-start(bf16[128,416,128]{2,1,0:T(8,128)(2,1)} %grams.1), calls=%async_computation.1 | async-start | bytes 27262976 | tf_op jit(solution)/shard_map/all_to_all | solution.py:263

commit v2 on v1

--- a/solution.py
+++ b/solution.py
@@ -11,6 +11,7 @@
 NS_ITERS = 5
 LOC_SCALE = 48.0
 AXES = ("lon", "lat")
+MESH = pl.DeviceIdType.MESH
 F32 = jnp.float32
 BF16 = jnp.bfloat16
 
@@ -45,12 +46,69 @@
     out_ref[8:16, :] += total
 
 
-def gram_kernel(per, lat_devices, lon_patches, lat_patches, code_ref, anom_ref, ext_ref, rinv_ref,
-                lon_ref, lat_ref, out_ref):
-    count = out_ref.shape[0]
-    first = pl.program_id(0) * count
+def coordinates():
+    lon, lat = lax.axis_index("lon"), lax.axis_index("lat")
+    return lat // 4, lon // 2, lat % 4, lon % 2
+
+
+def device_at(x, y, z, core):
+    return (y * 2 + core, x * 4 + z)
+
+
+def units_wait(ref, sem):
+    pltpu.make_async_copy(ref, ref, sem).wait()
+
+
+LINE_PEERS = [(0, 0, 0, 1)] + [
+    tuple(step if axis == a else 0 for a in range(3)) + (core,)
+    for axis in range(3)
+    for step in (1, 2, 3)
+    for core in (0, 1)
+]
+PLANE_PEERS = [
+    (dx, dy, dz, 0)
+    for dx in range(4)
+    for dy in range(4)
+    for dz in range(4)
+    if 0 < (dx != 0) + (dy != 0) + (dz != 0) < 3
+]
+
+
+def shifted(me, offset):
+    x, y, z, core = me
+    dx, dy, dz, dc = offset
+    return ((x + dx) % 4, (y + dy) % 4, (z + dz) % 4, (core + dc) % 2)
+
+
+def greet(me, offsets):
+    barrier = pltpu.get_barrier_semaphore()
+    for offset in offsets:
+        pl.semaphore_signal(
+            barrier, inc=1, device_id=device_at(*shifted(me, offset)), device_id_type=MESH
+        )
+    pl.semaphore_wait(barrier, len(offsets))
+
+
+def remote(src, dst, send, recv, target):
+    return pltpu.make_async_remote_copy(
+        src_ref=src,
+        dst_ref=dst,
+        send_sem=send,
+        recv_sem=recv,
+        device_id=device_at(*target),
+        device_id_type=MESH,
+    )
+
+
+def gram_kernel(per, lon_patches, lat_patches, code_ref, table_ref, anom_ref, ext_ref, rinv_ref,
+                lon_ref, lat_ref, got_ref, codes_ref, stage, send, recv, own, send2, recv2, own2):
+    me = coordinates()
+    xm, ym, zm, cm = me
+    mine = (zm, xm, ym)
     members = anom_ref.shape[1]
     half = members // 2
+    third = (half + 8) // 3
+    requesters = stage.shape[0]
     grid_lon = float(8 * lon_patches * PSIDE)
     row = lax.broadcasted_iota(jnp.int32, (half, members), 0)
     lane = lax.broadcasted_iota(jnp.int32, (half, members), 1)
@@ -58,17 +116,56 @@
     on_diag = row == lane
     row8 = lax.broadcasted_iota(jnp.int32, (8, members), 0)
 
+    greet(me, LINE_PEERS)
+    for q in range(3):
+        source = mine[q] * 2 + cm
+        for step in range(4):
+            for core in range(2):
+                offset = [0, 0, 0, core]
+                offset[(2, 0, 1)[q]] = step
+                dst = codes_ref.at[q, source]
+                if step == 0 and core == 0:
+                    pltpu.make_async_copy(table_ref, dst, own2.at[q]).start()
+                else:
+                    remote(table_ref, dst, send2, recv2, shifted(me, offset)).start()
+
+    def offset_of(i):
+        dx = i % 4
+        dy = (i + i // 4) % 4
+        dz = (i + i // 16) % 4
+        return dx, dy, dz, i // 64
+
+    def ship(i):
+        dx, dy, dz, dc = offset_of(i)
+        x, y, z, core = shifted(me, (dx, dy, dz, dc))
+        targets = ((xm, ym, z, core), (x, ym, zm, core), (xm, y, zm, core))
+        places = (x * 4 + y, y * 4 + z, x * 4 + z)
+        for q, moved in enumerate((dz, dx, dy)):
+            src = stage.at[i, q]
+            dst = got_ref.at[q, mine[q] * 2 + cm, places[q]]
+            stays = (moved == 0) & (dc == 0)
+
+            @pl.when(stays)
+            def _():
+                pltpu.make_async_copy(src, dst, own).start()
+
+            @pl.when(jnp.logical_not(stays))
+            def _():
+                remote(src, dst, send, recv, targets[q]).start()
+
     def one(i, carry):
-        who = first + i
-        diags = jnp.zeros((8, members), F32)
-        projs = jnp.zeros((8, members), F32)
+        x, y, z, core = shifted(me, offset_of(i))
+        lon_device = y * 2 + core
+        lat_device = x * 4 + z
+        who = lon_device * 16 + lat_device
+        pieces = []
         for s in range(per):
             code = code_ref[who * 8 + s]
             valid = code % 2
             patch = (code // 2) % 16
             held = code // 32
-            cl = ((who // lat_devices) * lon_patches + patch // lat_patches) * PSIDE
-            ct = ((who % lat_devices) * lat_patches + patch % lat_patches) * PSIDE
+            cl = (lon_device * lon_patches + patch // lat_patches) * PSIDE
+            ct = (lat_device * lat_patches + patch % lat_patches) * PSIDE
             cl = cl.astype(F32) + (PSIDE - 1) / 2.0
             ct = ct.astype(F32) + (PSIDE - 1) / 2.0
             gap = jnp.abs(lon_ref[pl.ds(held, 1), :] - cl)
@@ -86,41 +183,105 @@
             )
             top = full[:half, :]
             low = pltpu.roll(full[half:members, :], half, 1)
-            out_ref[i, s * half : (s + 1) * half, :] = jnp.where(keep, top, low).astype(BF16)
             diag = jnp.sum(jnp.where(on_diag, low, 0.0), axis=0, keepdims=True)
             proj = jnp.sum(full[members : members + 8, :], axis=0, keepdims=True)
-            diags = jnp.where(row8 == s, diag, diags)
-            projs = jnp.where(row8 == s, proj, projs)
-        high = projs.astype(BF16).astype(F32)
-        extra = jnp.concatenate([diags, high, projs - high, jnp.zeros_like(high)], axis=0)
-        out_ref[i, per * half : per * half + 32, :] = extra.astype(BF16)
+            high = proj.astype(BF16).astype(F32)
+            extra = jnp.where(
+                row8 == 0, diag, jnp.where(row8 == 1, high, jnp.where(row8 == 2, proj - high, 0.0))
+            )
+            pieces.append(jnp.concatenate([jnp.where(keep, top, low), extra], axis=0))
+        for q in range(3):
+            for s in range(0, per, 2):
+                both = jnp.concatenate(
+                    [pieces[s][q * third : (q + 1) * third], pieces[s + 1][q * third : (q + 1) * third]],
+                    axis=0,
+                )
+                stage[i, q, s * third : (s + 2) * third, :] = both.astype(BF16)
+
+        @pl.when(i > 0)
+        def _():
+            ship(i - 1)
+
         return carry
 
-    lax.fori_loop(0, count, one, 0)
-
-
-def gather_kernel(per, patch_ref, got_ref, acc_ref):
-    count = got_ref.shape[0]
-    step = pl.program_id(0)
-    half = (got_ref.shape[1] - 32) // per
-
-    @pl.when(step == 0)
+    lax.fori_loop(0, requesters, one, 0)
+    ship(requesters - 1)
+
+    for q in range(3):
+        pltpu.make_async_copy(table_ref, codes_ref.at[q, 0], own2.at[q]).wait()
+    units_wait(codes_ref.at[:, 0:7], send2)
+    units_wait(codes_ref.at[:, 0:7], recv2)
+    units_wait(stage.at[0:16], own)
+    units_wait(stage.at[0:112], send)
+    units_wait(got_ref.at[:, 0:7], recv)
+
+
+def add_kernel(per, me_ref, codes_ref, got_ref, out_ref, acc):
+    q = pl.program_id(0)
+    place = pl.program_id(1)
+    major, minor = place // 4, place % 4
+    x = jnp.where(q == 1, me_ref[0], major)
+    y = jnp.where(q == 2, me_ref[1], jnp.where(q == 0, minor, major))
+    z = jnp.where(q == 0, me_ref[2], minor)
+    who = (y * 2 + me_ref[3]) * 16 + x * 4 + z
+    third = got_ref.shape[3] // per
+    acc[...] = jnp.zeros_like(acc)
+    for source in range(got_ref.shape[1]):
+        for s in range(0, per, 2):
+            both = got_ref[0, source, 0, s * third : (s + 2) * third, :].astype(F32)
+            for t in range(2):
+                where = who * 8 + s + t
+                code = codes_ref[0, source * 8 + where // 128, where % 128]
+                start = pl.multiple_of(((code // 2) % 16) * third, 8)
+                acc[pl.ds(start, third), :] += both[t * third : (t + 1) * third]
+
+    @pl.when(q == 2)
     def _():
-        acc_ref[...] = jnp.zeros_like(acc_ref)
-
-    def one(i, carry):
-        extra = got_ref[i, per * half :, :].astype(F32)
-        proj = extra[8:16, :] + extra[16:24, :]
-        for s in range(per):
-            patch = patch_ref[(step * count + i) * per + s]
-            acc_ref[patch, 0:half, :] += got_ref[i, s * half : (s + 1) * half, :].astype(F32)
-            pair = jnp.concatenate(
-                [extra[s : s + 1, :], proj[s : s + 1, :], jnp.zeros((6, proj.shape[1]), F32)], axis=0
+        row8 = lax.broadcasted_iota(jnp.int32, (8, acc.shape[1]), 0)
+        for p in range(acc.shape[0] // third):
+            rows = acc[p * third + 16 : p * third + 24, :]
+            proj = rows[1:2, :] + rows[2:3, :]
+            high = proj.astype(BF16).astype(F32)
+            acc[p * third + 16 : p * third + 24, :] = jnp.where(
+                row8 == 1, high, jnp.where(row8 == 2, proj - high, rows)
             )
-            acc_ref[patch, half : half + 8, :] += pair
-        return carry
-
-    lax.fori_loop(0, count, one, 0)
+
+    out_ref[0, 0] = acc[...].astype(BF16)
+
+
+def plane_kernel(dense_ref, acc_ref, held, send, recv, own):
+    me = coordinates()
+    xm, ym, zm, cm = me
+    places = (xm * 4 + ym, ym * 4 + zm, xm * 4 + zm)
+    third = dense_ref.shape[2] // acc_ref.shape[0]
+    greet(me, PLANE_PEERS)
+    for k in range(16):
+        first, second = k % 4, (k + k // 4) % 4
+        for q in range(3):
+            offset = ((first, second, 0, 0), (0, first, second, 0), (first, 0, second, 0))[q]
+            x, y, z, core = shifted(me, offset)
+            place = (x * 4 + y, y * 4 + z, x * 4 + z)[q]
+            src = dense_ref.at[q, place]
+            dst = held.at[q, places[q]]
+            if first == 0 and second == 0:
+                pltpu.make_async_copy(src, dst, own.at[q]).start()
+            else:
+                remote(src, dst, send, recv.at[q], (x, y, z, core)).start()
+    for q in range(3):
+        pltpu.make_async_copy(dense_ref.at[q, 0], held.at[q, 0], own.at[q]).wait()
+        units_wait(held.at[q, 0:15], recv.at[q])
+
+        def one(j, carry):
+            start = pl.multiple_of(j * 2 * third, 16)
+            total = held[q, 0, pl.ds(start, 2 * third), :].astype(F32)
+            for source in range(1, 16):
+                total += held[q, source, pl.ds(start, 2 * third), :].astype(F32)
+            acc_ref[2 * j, q * third : (q + 1) * third, :] = total[:third]
+            acc_ref[2 * j + 1, q * third : (q + 1) * third, :] = total[third:]
+            return carry
+
+        lax.fori_loop(0, acc_ref.shape[0] // 2, one, 0)
+    units_wait(held.at[:, 0:15], send)
 
 
 def halves(x):
@@ -171,7 +332,7 @@
     for q in range(count):
         _, inverse, scaling = state[q]
         inverse = inverse * (1.0 / jnp.sqrt(scaling))
-        proj = acc_ref[q, half + 1 : half + 2, :]
+        proj = acc_ref[q, half + 1 : half + 2, :] + acc_ref[q, half + 2 : half + 3, :]
         inverse2 = halves(inverse)
         mean = jnp.broadcast_to(proj, (8, members))
         mean = product(halves(mean), inverse2)
@@ -186,7 +347,6 @@
     state_pert, state_mean, obs_anom, innov, obs_rinv, obs_lon, obs_lat, block_list, block_count
 ):
     holders = lax.axis_size(AXES)
-    lat_devices = lax.axis_size("lat")
     lon_patches, lat_patches, fields, members, columns = state_pert.shape
     patches = lon_patches * lat_patches
     list_length = block_list.shape[2]
@@ -194,7 +354,6 @@
     slots = patches * list_length
     per = slots // holders
     half = members // 2
-    rows = per * half + 32
 
     step_blocks = 16
     sums, ext = pl.pallas_call(
@@ -241,39 +400,58 @@
     base = ((members - 1) / inflation).reshape(1)
     codes = asked.astype(jnp.int32).reshape(holders * 8)
 
-    turn = 8
-    whole3 = lambda i: (0, 0, 0)
-    whole2 = lambda i: (0, 0)
-    grams = pl.pallas_call(
-        functools.partial(gram_kernel, per, lat_devices, lon_patches, lat_patches),
-        grid=(holders // turn,),
+    third = (half + 8) // 3
+    got, tables = pl.pallas_call(
+        functools.partial(gram_kernel, per, lon_patches, lat_patches),
+        in_specs=[pl.BlockSpec(memory_space=pltpu.SMEM), pl.BlockSpec(memory_space=pl.ANY)]
+        + [pl.BlockSpec(memory_space=pltpu.VMEM)] * 5,
+        out_specs=[pl.BlockSpec(memory_space=pl.ANY)] * 2,
+        out_shape=[
+            jax.ShapeDtypeStruct((3, 8, 16, per * third, members), BF16),
+            jax.ShapeDtypeStruct((3, 8, 8, 128), jnp.int32),
+        ],
+        scratch_shapes=[
+            pltpu.VMEM((holders, 3, per * third, members), BF16),
+            pltpu.SemaphoreType.DMA,
+            pltpu.SemaphoreType.DMA,
+            pltpu.SemaphoreType.DMA,
+            pltpu.SemaphoreType.DMA,
+            pltpu.SemaphoreType.DMA,
+            pltpu.SemaphoreType.DMA((3,)),
+        ],
+        compiler_params=pltpu.CompilerParams(collective_id=0, has_side_effects=True),
+        name="grams",
+    )(codes, codes.reshape(8, 128), obs_anom, ext, obs_rinv, obs_lon.astype(F32), obs_lat.astype(F32))
+
+    x, y, z, core = coordinates()
+    dense = pl.pallas_call(
+        functools.partial(add_kernel, per),
+        grid=(3, 16),
         in_specs=[
             pl.BlockSpec(memory_space=pltpu.SMEM),
-            pl.BlockSpec((held_blocks, members, block_obs), whole3),
-            pl.BlockSpec((held_blocks, 16, block_obs), whole3),
-            pl.BlockSpec((held_blocks, block_obs), whole2),
-            pl.BlockSpec((held_blocks, block_obs), whole2),
-            pl.BlockSpec((held_blocks, block_obs), whole2),
-        ],
-        out_specs=pl.BlockSpec((turn, rows, members), lambda i: (i, 0, 0)),
-        out_shape=jax.ShapeDtypeStruct((holders, rows, members), BF16),
-        name="grams",
-    )(codes, obs_anom, ext, obs_rinv, obs_lon.astype(F32), obs_lat.astype(F32))
-
-    got = lax.all_to_all(grams, AXES, split_axis=0, concat_axis=0, tiled=True)
-
-    patch_of = (requests // 2) % 16
+            pl.BlockSpec((1, 64, 128), lambda q, i: (q, 0, 0), memory_space=pltpu.SMEM),
+            pl.BlockSpec((1, 8, 1, per * third, members), lambda q, i: (q, 0, i, 0, 0)),
+        ],
+        out_specs=pl.BlockSpec((1, 1, patches * third, members), lambda q, i: (q, i, 0, 0)),
+        out_shape=jax.ShapeDtypeStruct((3, 16, patches * third, members), BF16),
+        scratch_shapes=[pltpu.VMEM((patches * third, members), F32)],
+        name="adds",
+    )(jnp.stack([x, y, z, core]), tables.reshape(3, 64, 128), got)
+
     acc = pl.pallas_call(
-        functools.partial(gather_kernel, per),
-        grid=(holders // turn,),
-        in_specs=[
-            pl.BlockSpec(memory_space=pltpu.SMEM),
-            pl.BlockSpec((turn, rows, members), lambda i: (i, 0, 0)),
-        ],
-        out_specs=pl.BlockSpec((patches, half + 8, members), whole3),
+        plane_kernel,
+        in_specs=[pl.BlockSpec(memory_space=pl.ANY)],
+        out_specs=pl.BlockSpec(memory_space=pltpu.VMEM),
         out_shape=jax.ShapeDtypeStruct((patches, half + 8, members), F32),
-        name="gather",
-    )(patch_of, got)
+        scratch_shapes=[
+            pltpu.VMEM((3, 16, patches * third, members), BF16),
+            pltpu.SemaphoreType.DMA,
+            pltpu.SemaphoreType.DMA((3,)),
+            pltpu.SemaphoreType.DMA((3,)),
+        ],
+        compiler_params=pltpu.CompilerParams(collective_id=1, has_side_effects=True),
+        name="planes",
+    )(dense)
 
     pair = 2
     updated = pl.pallas_call(

time: 324 us -> 223 us (0.69)
  waiting for transfers between devices: 190 us -> 6.93 us
  Pallas kernels: 104 us -> 190 us
  starting transfers between devices: 17.3 us -> 11.5 us
    all_to_all x1 -> x0, waiting for transfers between devices: 182 us -> none  [on_device(): got = lax.all_to_all(grams, AXES, split_axis=0, concat_axis=0, tiled=True)]
    pallas_call x2 -> x3, Pallas kernels: 71.4 us -> 157 us  [the longest x1 74.5 us: on_device(): pl.pallas_call(functools.partial(gram_kernel, per, lon_patches, lat_patch...]
    all_to_all x1 -> x0, starting transfers between devices: 5.82 us -> none  [on_device(): got = lax.all_to_all(grams, AXES, split_axis=0, concat_axis=0, tiled=True)]
  transfers between devices with their start and end apart: 2 -> 1, of which waited for: 2 -> 1; matrix products, arithmetic and copies ran while one was open for 1% -> 1% of each run, Pallas kernels for 0% -> 0%
where the time goes in v2:
time: 223 us; the launch traced here: 222 us
  Pallas kernels  190 us (85%)
  starting transfers between devices  11.5 us (5%)
  other arithmetic  6.94 us (3%)
  waiting for transfers between devices  6.93 us (3%)
  local copies, waits for them, and re-layouts  4.01 us (2%)
    pallas_call x1, Pallas kernels, on_device(): pl.pallas_call(functools.partial(gram_kernel, per, lon_patches, lat_patch...  74.5 us
    pallas_call x1, Pallas kernels, on_device(): pl.pallas_call(plane_kernel, in_specs=[pl.BlockSpec(memory_space=pl.ANY)]...  44 us
    pallas_call x1, Pallas kernels, on_device(): pl.pallas_call(functools.partial(add_kernel, per), grid=(3, 16), in_specs...  38.9 us
    pallas_call x1, Pallas kernels, on_device(): pl.pallas_call(update_kernel, grid=(patches // pair,), in_specs=[pl.Block...  23.9 us
    all_to_all x1, starting transfers between devices, on_device(): lax.all_to_all(message, AXES, split_axis=0, concat_axis=0, tiled=True)  11.5 us
    pallas_call x1, Pallas kernels, on_device(): pl.pallas_call(totals_kernel, grid=(held_blocks // step_blocks,), in_spec...  8.75 us
    all_to_all x1, waiting for transfers between devices, on_device(): lax.all_to_all(message, AXES, split_axis=0, concat_axis=0, tiled=True)  6.93 us
  transfers between devices with their start and end apart: 1, of which 1 were waited for; matrix products, arithmetic and copies ran while one was open for 1% of the time, Pallas kernels for 0%

profile of v2, /device:TPU:1, one launch (start us, length us, event | category | flops | bytes accessed | tf_op | source)
XLA Modules:
  0.0 221.5 jit_solution(15075618580385612918)
XLA Ops:
  0.0 0.7 broadcast_divide_fusion
  0.7 0.7 sign_compare_fusion
  1.4 0.1 div.52
  1.5 0.1 ne.104
  1.6 0.1 rem.78
  1.7 0.8 copy.18
  2.4 0.1 reshape.124
  2.5 0.1 broadcast_in_dim.16
  2.6 0.1 reshape.125
  2.7 0.4 convert_reduce_fusion
  3.1 0.3 select_reduce_fusion
  3.4 0.1 convert_element_type.36
  3.5 0.0 copy-start
  3.6 8.8 %totals.1 = (f32[16,128]{1,0:T(8,128)}, bf16[192,16,128]{2,1,0:T(8,128)(2,1)}) custom-call(bf16[192,128,128]{2,1,0:T(8,128)(2,1)} %anom_ref.3, f32[192,128]{1,0:T(8,128)} %rinv_ref.3, f32[192,128]{1,0:T(8,128)} %innov_ref.1), custom_call_target="tpu_custom_call" | custom-call | tf_op jit(solution)/shard_map/totals/pallas_call | solution.py:359
  12.3 1.3 slice_reduce_fusion.2
  14.3 0.6 pad_maximum_fusion.1
  14.9 0.6 pad_maximum_fusion
  15.5 11.5 %all-to-all-start = ((f32[128,1,8]{2,1,0:T(1,128)}), f32[128,1,8]{2,1,0:T(1,128)S(1)}, u32[]{:S(2)}, u32[]{:S(2)}) async-start(f32[128,1,8]{2,1,0:T(1,128)} %bitcast.3), calls=%async_computation | async-start | bytes 131072 | tf_op jit(solution)/shard_map/all_to_all | solution.py:397
  27.1 0.6 pad_add_fusion.me_ref
  27.7 0.6 convert_element_type.40.lon_ref
  28.3 0.7 convert_element_type.41.lat_ref
  29.0 0.7 copy.20
  29.7 6.9 %all-to-all-done = f32[128,1,8]{2,1,0:T(1,128)S(1)} async-done(((f32[128,1,8]{2,1,0:T(1,128)}), f32[128,1,8]{2,1,0:T(1,128)S(1)}, u32[]{:S(2)}, u32[]{:S(2)}) %all-to-all-start) | async-done | bytes 4128 | tf_op jit(solution)/shard_map/all_to_all | solution.py:397
  36.6 0.1 slice_reduce_fusion
  36.7 0.6 fusion.13
  37.3 0.2 convert_reduce_fusion.1
  37.5 0.7 convert_element_type.38.code_ref
  38.2 0.7 convert_element_type.39.table_ref
  38.9 74.5 %grams.1 = (bf16[3,8,16,144,128]{4,3,2,1,0:T(8,128)(2,1)}, s32[3,8,8,128]{3,2,1,0:T(8,128)}) custom-call(s32[1024]{0:T(1024)} %convert_element_type.38.code_ref, s32[8,128]{1,0:T(8,128)} %convert_element_type.39.table_ref, bf16[192,128,128]{2,1,0:T(8,128)(2,1)} %anom_ref.3, bf16[192,16,128]{2,1,0:T(8,128)(2,1)} %get-tuple-element.10.ext_ref, ...), custom_call_target="tpu_custom_call" | custom-call | tf_op jit(solution)/shard_map/grams/pallas_call | solution.py:404
  113.4 38.9 %adds.1.dense_ref = bf16[3,16,384,128]{3,2,1,0:T(8,128)(2,1)} custom-call(s32[4]{0:T(128)} %pad_add_fusion.me_ref, s32[3,64,128]{2,1,0:T(8,128)} %bitcast.19, bf16[3,8,16,144,128]{4,3,2,1,0:T(8,128)(2,1)} %get-tuple-element.12.got_ref), custom_call_target="tpu_custom_call" | custom-call | tf_op jit(solution)/shard_map/adds/pallas_call | solution.py:427
  152.3 44.0 %planes.1.acc_ref = f32[16,72,128]{2,1,0:T(8,128)} custom-call(bf16[3,16,384,128]{3,2,1,0:T(8,128)(2,1)} %adds.1.dense_ref), custom_call_target="tpu_custom_call" | custom-call | tf_op jit(solution)/shard_map/planes/pallas_call | solution.py:441
  197.6 23.9 %update.1 = f32[16,6,128,256]{3,2,1,0:T(8,128)} custom-call(f32[1]{0:T(128)S(6)} %div.55.base_ref, f32[16,72,128]{2,1,0:T(8,128)} %planes.1.acc_ref, bf16[16,6,128,256]{3,2,1,0:T(8,128)(2,1)} %bitcast.15, f32[16,6,256]{2,1,0:T(8,128)} %bitcast.17), custom_call_target="tpu_custom_call" | custom-call | tf_op jit(solution)/shard_map/update/pallas_call | solution.py:457
  (9 shorter events, 0.1 us)
Async XLA Ops:
  3.5 24.2 %copy-start.1 = (s32[192,128]{1,0:T(8,128)S(1)}, s32[192,128]{1,0:T(8,128)}, u32[]{:S(2)}) copy-start(s32[192,128]{1,0:T(8,128)} %param.14) | copy-start | bytes 294916
  3.5 24.8 %copy-start.2 = (s32[192,128]{1,0:T(8,128)S(1)}, s32[192,128]{1,0:T(8,128)}, u32[]{:S(2)}) copy-start(s32[192,128]{1,0:T(8,128)} %param.15) | copy-start | bytes 294916
  3.5 25.4 %copy-start = (f32[8,2,6,256]{3,1,2,0:T(2,128)S(1)}, f32[8,2,6,256]{3,1,2,0:T(2,128)}, u32[]{:S(2)}) copy-start(f32[8,2,6,256]{3,1,2,0:T(2,128)} %param.10) | copy-start | bytes 294916
  15.5 21.1 %all-to-all-start = ((f32[128,1,8]{2,1,0:T(1,128)}), f32[128,1,8]{2,1,0:T(1,128)S(1)}, u32[]{:S(2)}, u32[]{:S(2)}) async-start(f32[128,1,8]{2,1,0:T(1,128)} %bitcast.3), calls=%async_computation | async-start | bytes 131072 | tf_op jit(solution)/shard_map/all_to_all | solution.py:397

commit v3 on v2

--- a/solution.py
+++ b/solution.py
@@ -12,43 +12,50 @@
 LOC_SCALE = 48.0
 AXES = ("lon", "lat")
 MESH = pl.DeviceIdType.MESH
+CHAINS = 2
+PAIR = 8
 F32 = jnp.float32
 BF16 = jnp.bfloat16
 
 
-def totals_kernel(anom_ref, rinv_ref, innov_ref, out_ref, ext_ref):
-    step = pl.program_id(0)
-    blocks = anom_ref.shape[0]
-
-    @pl.when(step == 0)
-    def _():
-        out_ref[...] = jnp.zeros_like(out_ref)
-
+def totals_kernel(turn, anom_ref, rinv_ref, innov_ref, out_ref, ext_ref, held, sems):
+    blocks, _, width = anom_ref.shape
+    turns = blocks // turn
+
+    def copy(k):
+        return pltpu.make_async_copy(
+            anom_ref.at[pl.ds(k * turn, turn)], held.at[pl.ds(k * turn, turn)], sems.at[k]
+        )
+
+    for k in range(turns):
+        copy(k).start()
     innov = innov_ref[...]
-    rinv = rinv_ref[...]
-    high = innov.astype(BF16)
-    rest = innov - high.astype(F32)
-    mid = rest.astype(BF16)
-    low = (rest - mid.astype(F32)).astype(BF16)
+    high = innov.astype(BF16).astype(F32)
+    rest = innov - high
+    mid = rest.astype(BF16).astype(F32)
+    low = rest - mid
     ext = jnp.concatenate(
-        [high[:, None, :].astype(F32), mid[:, None, :].astype(F32), low[:, None, :].astype(F32)]
-        + [jnp.zeros((blocks, 13, innov.shape[1]), F32)],
-        axis=1,
+        [high[:, None, :], mid[:, None, :], low[:, None, :], jnp.zeros((blocks, 13, width), F32)], axis=1
     )
     ext_ref[...] = ext.astype(BF16)
-    out_ref[0:8, :] += jnp.sum((rinv * innov * innov).reshape(blocks // 8, 8, -1), axis=0)
-
-    total = jnp.zeros((8, innov.shape[1]), F32)
-    for b in range(blocks):
-        a = anom_ref[b].astype(F32)
-        squares = jnp.sum((a * a).reshape(-1, 8, a.shape[1]), axis=0)
-        total = total + squares * rinv[b : b + 1, :]
-    out_ref[8:16, :] += total
+    out_ref[0:8, :] = jnp.sum((rinv_ref[...] * innov * innov).reshape(blocks // 8, 8, width), axis=0)
+
+    def one(k, total):
+        copy(k).wait()
+        first = pl.multiple_of(k * turn, turn)
+        rinv = rinv_ref[pl.ds(first, turn), :]
+        for b in range(turn):
+            a = held[first + b].astype(F32)
+            squares = jnp.sum((a * a).reshape(-1, 8, width), axis=0)
+            total = total + squares * rinv[b : b + 1, :]
+        return total
+
+    out_ref[8:16, :] = lax.fori_loop(0, turns, one, jnp.zeros((8, width), F32))
 
 
 def coordinates():
     lon, lat = lax.axis_index("lon"), lax.axis_index("lat")
-    return lat // 4, lon // 2, lat % 4, lon % 2
+    return lax.div(lat, 4), lax.div(lon, 2), lax.rem(lat, 4), lax.rem(lon, 2)
 
 
 def device_at(x, y, z, core):
@@ -77,7 +84,10 @@
 def shifted(me, offset):
     x, y, z, core = me
     dx, dy, dz, dc = offset
-    return ((x + dx) % 4, (y + dy) % 4, (z + dz) % 4, (core + dc) % 2)
+    return tuple(
+        lax.rem(a + d, n) if not isinstance(d, int) or d else a
+        for a, d, n in ((x, dx, 4), (y, dy, 4), (z, dz, 4), (core, dc, 2))
+    )
 
 
 def greet(me, offsets):
@@ -130,10 +140,10 @@
                     remote(table_ref, dst, send2, recv2, shifted(me, offset)).start()
 
     def offset_of(i):
-        dx = i % 4
-        dy = (i + i // 4) % 4
-        dz = (i + i // 16) % 4
-        return dx, dy, dz, i // 64
+        dx = lax.rem(i, 4)
+        dy = lax.rem(i + lax.div(i, 4), 4)
+        dz = lax.rem(i + lax.div(i, 16), 4)
+        return dx, dy, dz, lax.div(i, 64)
 
     def ship(i):
         dx, dy, dz, dc = offset_of(i)
@@ -157,17 +167,16 @@
         x, y, z, core = shifted(me, offset_of(i))
         lon_device = y * 2 + core
         lat_device = x * 4 + z
-        who = lon_device * 16 + lat_device
+        who8 = (lon_device * 16 + lat_device) * 8
+        lon_first = lon_device * (lon_patches * PSIDE)
+        lat_first = lat_device * (lat_patches * PSIDE)
         pieces = []
         for s in range(per):
-            code = code_ref[who * 8 + s]
-            valid = code % 2
-            patch = (code // 2) % 16
-            held = code // 32
-            cl = (lon_device * lon_patches + patch // lat_patches) * PSIDE
-            ct = (lat_device * lat_patches + patch % lat_patches) * PSIDE
-            cl = cl.astype(F32) + (PSIDE - 1) / 2.0
-            ct = ct.astype(F32) + (PSIDE - 1) / 2.0
+            code = code_ref[who8 + s]
+            valid = code & 1
+            held = code >> 8
+            cl = (lon_first + (code & 112)).astype(F32) + (PSIDE - 1) / 2.0
+            ct = (lat_first + ((code & 128) >> 3)).astype(F32) + (PSIDE - 1) / 2.0
             gap = jnp.abs(lon_ref[pl.ds(held, 1), :] - cl)
             gap = jnp.minimum(gap, grid_lon - gap)
             other = lat_ref[pl.ds(held, 1), :] - ct
@@ -205,7 +214,7 @@
         return carry
 
     lax.fori_loop(0, requesters, one, 0)
-    ship(requesters - 1)
+    ship(jnp.int32(requesters - 1))
 
     for q in range(3):
         pltpu.make_async_copy(table_ref, codes_ref.at[q, 0], own2.at[q]).wait()
@@ -216,37 +225,56 @@
     units_wait(got_ref.at[:, 0:7], recv)
 
 
-def add_kernel(per, me_ref, codes_ref, got_ref, out_ref, acc):
-    q = pl.program_id(0)
-    place = pl.program_id(1)
-    major, minor = place // 4, place % 4
-    x = jnp.where(q == 1, me_ref[0], major)
-    y = jnp.where(q == 2, me_ref[1], jnp.where(q == 0, minor, major))
-    z = jnp.where(q == 0, me_ref[2], minor)
-    who = (y * 2 + me_ref[3]) * 16 + x * 4 + z
-    third = got_ref.shape[3] // per
-    acc[...] = jnp.zeros_like(acc)
-    for source in range(got_ref.shape[1]):
-        for s in range(0, per, 2):
-            both = got_ref[0, source, 0, s * third : (s + 2) * third, :].astype(F32)
-            for t in range(2):
-                where = who * 8 + s + t
-                code = codes_ref[0, source * 8 + where // 128, where % 128]
-                start = pl.multiple_of(((code // 2) % 16) * third, 8)
-                acc[pl.ds(start, third), :] += both[t * third : (t + 1) * third]
-
-    @pl.when(q == 2)
-    def _():
-        row8 = lax.broadcasted_iota(jnp.int32, (8, acc.shape[1]), 0)
-        for p in range(acc.shape[0] // third):
-            rows = acc[p * third + 16 : p * third + 24, :]
-            proj = rows[1:2, :] + rows[2:3, :]
-            high = proj.astype(BF16).astype(F32)
-            acc[p * third + 16 : p * third + 24, :] = jnp.where(
-                row8 == 1, high, jnp.where(row8 == 2, proj - high, rows)
-            )
-
-    out_ref[0, 0] = acc[...].astype(BF16)
+def add_kernel(per, me_ref, starts_ref, got_ref, out_ref, held, made, sems, out_sems, *accs):
+    sources, places = held.shape[1:3]
+    third = held.shape[3] // per
+    chains = len(accs)
+    row8 = lax.broadcasted_iota(jnp.int32, (8, held.shape[4]), 0)
+
+    def copy(q, source):
+        return pltpu.make_async_copy(got_ref.at[q, source], held.at[q, source], sems.at[q, source])
+
+    for q in range(3):
+        for source in range(sources):
+            copy(q, source).start()
+    for q in range(3):
+        for source in range(sources):
+            copy(q, source).wait()
+
+        def one(place, carry):
+            major, minor = lax.div(place, 4), lax.rem(place, 4)
+            x = me_ref[0] if q == 1 else major
+            y = me_ref[1] if q == 2 else (minor if q == 0 else major)
+            z = me_ref[2] if q == 0 else minor
+            first = ((y * 2 + me_ref[3]) * 16 + x * 4 + z) * 8
+            for acc in accs:
+                acc[...] = jnp.zeros_like(acc)
+            for source in range(sources):
+                for s in range(0, per, 2):
+                    both = held[q, source, place, s * third : (s + 2) * third, :].astype(F32)
+                    for t in range(2):
+                        start = pl.multiple_of(starts_ref[q, source, first + s + t], 8)
+                        accs[(s + t) % chains][pl.ds(start, third), :] += both[t * third : (t + 1) * third]
+            if q < 2:
+                made[q, place] = functools.reduce(lambda a, b: a + b, [acc[...] for acc in accs]).astype(BF16)
+            else:
+                for p in range(0, accs[0].shape[0] // third, 2):
+                    rows = slice(p * third, (p + 2) * third)
+                    total = functools.reduce(lambda a, b: a + b, [acc[rows, :] for acc in accs])
+                    parts = []
+                    for t in range(2):
+                        top = total[t * third : t * third + 16]
+                        last = total[t * third + 16 : (t + 1) * third]
+                        proj = last[1:2, :] + last[2:3, :]
+                        high = proj.astype(BF16).astype(F32)
+                        parts += [top, jnp.where(row8 == 1, high, jnp.where(row8 == 2, proj - high, last))]
+                    made[q, place, rows, :] = jnp.concatenate(parts, axis=0).astype(BF16)
+            return carry
+
+        lax.fori_loop(0, places, one, 0)
+        pltpu.make_async_copy(made.at[q], out_ref.at[q], out_sems.at[q]).start()
+    for q in range(3):
+        pltpu.make_async_copy(made.at[q], out_ref.at[q], out_sems.at[q]).wait()
 
 
 def plane_kernel(dense_ref, acc_ref, held, send, recv, own):
@@ -289,17 +317,44 @@
     return high, (x - high.astype(F32)).astype(BF16)
 
 
-def product(left, right):
+def stacked(pairs):
+    return jnp.concatenate([part for pair in pairs for part in pair], axis=0)
+
+
+def products(lefts, right):
     n = right[0].shape[1]
-    lhs = jnp.concatenate([left[0], left[1]], axis=1)
-    upper = jnp.concatenate([right[0], right[1]], axis=1)
-    lower = jnp.concatenate([right[0], jnp.zeros_like(right[1])], axis=1)
-    both = jnp.dot(lhs, jnp.concatenate([upper, lower], axis=0), preferred_element_type=F32)
-    return both[:, :n] + both[:, n:]
-
-
-def update_kernel(base_ref, acc_ref, pert_ref, mean_ref, out_ref):
-    count, fields, members, _ = pert_ref.shape
+    rows = lefts[0][0].shape[0]
+    both = jnp.dot(stacked(lefts), jnp.concatenate(right, axis=1), preferred_element_type=F32)
+    found = []
+    for k in range(len(lefts)):
+        high = both[2 * k * rows : (2 * k + 1) * rows]
+        low = both[(2 * k + 1) * rows : (2 * k + 2) * rows]
+        found.append(high[:, :n] + (high[:, n:] + low[:, :n]))
+    return found
+
+
+def update_kernel(count, base_ref, acc_ref, pert_ref, mean_ref, out_ref, perts, made, sems, out_sems):
+    patches, fields, members, _ = pert_ref.shape
+
+    def take(p):
+        return pltpu.make_async_copy(pert_ref.at[p], perts.at[p], sems.at[p])
+
+    def put(p):
+        return pltpu.make_async_copy(made.at[p], out_ref.at[p], out_sems.at[p])
+
+    for p in range(patches):
+        take(p).start()
+
+    def one(g, carry):
+        update_patches(g * count, count, fields, members, base_ref, acc_ref, mean_ref, perts, made, take, put)
+        return carry
+
+    lax.fori_loop(0, patches // count, one, 0)
+    for p in range(patches):
+        put(p).wait()
+
+
+def update_patches(first, count, fields, members, base_ref, acc_ref, mean_ref, perts, made, take, put):
     half = members // 2
     row = lax.broadcasted_iota(jnp.int32, (members, members), 0)
     lane = lax.broadcasted_iota(jnp.int32, (members, members), 1)
@@ -309,38 +364,40 @@
     base = base_ref[0]
     state = []
     for q in range(count):
-        packed = acc_ref[q, 0:half, :]
+        packed = acc_ref[first + q, 0:half, :]
         top = jnp.where((c >= half) | (r > c), packed, 0.0)
         low = pltpu.roll(jnp.where((c < half) & (r < c), packed, 0.0), half, 1)
         part = jnp.concatenate([top, low], axis=0)
         own = jnp.sum(jnp.where(r == c, packed, 0.0), axis=0, keepdims=True)
-        own = own + pltpu.roll(acc_ref[q, half : half + 1, :], half, 1)
+        own = own + pltpu.roll(acc_ref[first + q, half : half + 1, :], half, 1)
         system = part + part.T + jnp.where(row == lane, own + base, 0.0)
         scaling = jnp.sqrt(jnp.sum(jnp.sum(system * system, axis=0, keepdims=True), axis=1, keepdims=True))
         root = system / scaling
         factor = 1.5 * eye - 0.5 * root
-        state.append([product(halves(root), halves(factor)), factor, scaling])
+        state.append([products([halves(root)], halves(factor))[0], factor, scaling])
     for it in range(1, NS_ITERS):
         for q in range(count):
             root, inverse, _ = state[q]
-            inverse2 = halves(inverse)
-            factor = 1.5 * eye - 0.5 * product(inverse2, halves(root))
-            factor2 = halves(factor)
-            state[q][1] = product(factor2, inverse2)
+            root2, inverse2 = halves(root), halves(inverse)
+            factor = 1.5 * eye - 0.5 * products([inverse2], root2)[0]
             if it < NS_ITERS - 1:
-                state[q][0] = product(factor2, halves(root))
+                state[q][:2] = products([root2, inverse2], halves(factor))
+            else:
+                state[q][1] = products([inverse2], halves(factor))[0]
     for q in range(count):
         _, inverse, scaling = state[q]
         inverse = inverse * (1.0 / jnp.sqrt(scaling))
-        proj = acc_ref[q, half + 1 : half + 2, :] + acc_ref[q, half + 2 : half + 3, :]
+        proj = acc_ref[first + q, half + 1 : half + 2, :] + acc_ref[first + q, half + 2 : half + 3, :]
         inverse2 = halves(inverse)
-        mean = jnp.broadcast_to(proj, (8, members))
-        mean = product(halves(mean), inverse2)
-        mean = product(halves(mean), inverse2)[0:1, :]
+        mean = jnp.broadcast_to(proj, (16, members))
+        mean = products([halves(mean)], inverse2)[0]
+        mean = products([halves(mean)], inverse2)[0][0:1, :]
         weights = (float(members - 1) ** 0.5 * inverse + mean).astype(BF16)
+        take(first + q).wait()
         for f in range(fields):
-            change = jnp.dot(weights, pert_ref[q, f], preferred_element_type=F32)
-            out_ref[q, f] = mean_ref[q, f : f + 1, :] + change
+            change = jnp.dot(weights, perts[first + q, f], preferred_element_type=F32)
+            made[first + q, f] = mean_ref[first + q, f : f + 1, :] + change
+        put(first + q).start()
 
 
 def on_device(
@@ -355,22 +412,21 @@
     per = slots // holders
     half = members // 2
 
-    step_blocks = 16
+    vmem = pl.BlockSpec(memory_space=pltpu.VMEM)
+    smem = pl.BlockSpec(memory_space=pltpu.SMEM)
+    anywhere = pl.BlockSpec(memory_space=pl.ANY)
+    turn = 16
     sums, ext = pl.pallas_call(
-        totals_kernel,
-        grid=(held_blocks // step_blocks,),
-        in_specs=[
-            pl.BlockSpec((step_blocks, members, block_obs), lambda i: (i, 0, 0)),
-            pl.BlockSpec((step_blocks, block_obs), lambda i: (i, 0)),
-            pl.BlockSpec((step_blocks, block_obs), lambda i: (i, 0)),
-        ],
-        out_specs=[
-            pl.BlockSpec((16, block_obs), lambda i: (0, 0)),
-            pl.BlockSpec((step_blocks, 16, block_obs), lambda i: (i, 0, 0)),
-        ],
+        functools.partial(totals_kernel, turn),
+        in_specs=[anywhere, vmem, vmem],
+        out_specs=[vmem, vmem],
         out_shape=[
             jax.ShapeDtypeStruct((16, block_obs), F32),
             jax.ShapeDtypeStruct((held_blocks, 16, block_obs), BF16),
+        ],
+        scratch_shapes=[
+            pltpu.VMEM((held_blocks, members, block_obs), BF16),
+            pltpu.SemaphoreType.DMA((held_blocks // turn,)),
         ],
         name="totals",
     )(obs_anom, obs_rinv, innov)
@@ -382,7 +438,8 @@
     slot = jnp.arange(slots)
     patch = slot // list_length
     valid = (slot % list_length < jnp.repeat(block_count.reshape(patches), list_length)).astype(jnp.int32)
-    code = ((wanted % held_blocks) * 16 + patch) * 2 + valid
+    patch_lon, patch_lat = patch // lat_patches, patch % lat_patches
+    code = (wanted % held_blocks) * 256 + patch_lat * 128 + patch_lon * PSIDE + valid
     earlier = (holder[:, None] == holder[None, :]) & (slot[None, :] < slot[:, None])
     rank = jnp.sum(earlier.astype(jnp.int32), axis=1)
     bucket = holder * per + rank
@@ -401,6 +458,7 @@
     codes = asked.astype(jnp.int32).reshape(holders * 8)
 
     third = (half + 8) // 3
+    starts = (((codes >> 4) & 7) * lat_patches + ((codes >> 7) & 1)) * third
     got, tables = pl.pallas_call(
         functools.partial(gram_kernel, per, lon_patches, lat_patches),
         in_specs=[pl.BlockSpec(memory_space=pltpu.SMEM), pl.BlockSpec(memory_space=pl.ANY)]
@@ -421,22 +479,23 @@
         ],
         compiler_params=pltpu.CompilerParams(collective_id=0, has_side_effects=True),
         name="grams",
-    )(codes, codes.reshape(8, 128), obs_anom, ext, obs_rinv, obs_lon.astype(F32), obs_lat.astype(F32))
+    )(codes, starts.reshape(8, 128), obs_anom, ext, obs_rinv, obs_lon.astype(F32), obs_lat.astype(F32))
 
     x, y, z, core = coordinates()
     dense = pl.pallas_call(
         functools.partial(add_kernel, per),
-        grid=(3, 16),
-        in_specs=[
-            pl.BlockSpec(memory_space=pltpu.SMEM),
-            pl.BlockSpec((1, 64, 128), lambda q, i: (q, 0, 0), memory_space=pltpu.SMEM),
-            pl.BlockSpec((1, 8, 1, per * third, members), lambda q, i: (q, 0, i, 0, 0)),
-        ],
-        out_specs=pl.BlockSpec((1, 1, patches * third, members), lambda q, i: (q, i, 0, 0)),
+        in_specs=[smem, smem, anywhere],
+        out_specs=anywhere,
         out_shape=jax.ShapeDtypeStruct((3, 16, patches * third, members), BF16),
-        scratch_shapes=[pltpu.VMEM((patches * third, members), F32)],
+        scratch_shapes=[
+            pltpu.VMEM((3, 8, 16, per * third, members), BF16),
+            pltpu.VMEM((3, 16, patches * third, members), BF16),
+            pltpu.SemaphoreType.DMA((3, 8)),
+            pltpu.SemaphoreType.DMA((3,)),
+        ]
+        + [pltpu.VMEM((patches * third, members), F32)] * CHAINS,
         name="adds",
-    )(jnp.stack([x, y, z, core]), tables.reshape(3, 64, 128), got)
+    )(jnp.stack([x, y, z, core]), tables.reshape(3, 8, 1024), got)
 
     acc = pl.pallas_call(
         plane_kernel,
@@ -453,18 +512,17 @@
         name="planes",
     )(dense)
 
-    pair = 2
     updated = pl.pallas_call(
-        update_kernel,
-        grid=(patches // pair,),
-        in_specs=[
-            pl.BlockSpec(memory_space=pltpu.SMEM),
-            pl.BlockSpec((pair, half + 8, members), lambda i: (i, 0, 0)),
-            pl.BlockSpec((pair, fields, members, columns), lambda i: (i, 0, 0, 0)),
-            pl.BlockSpec((pair, fields, columns), lambda i: (i, 0, 0)),
-        ],
-        out_specs=pl.BlockSpec((pair, fields, members, columns), lambda i: (i, 0, 0, 0)),
+        functools.partial(update_kernel, PAIR),
+        in_specs=[smem, vmem, anywhere, vmem],
+        out_specs=anywhere,
         out_shape=jax.ShapeDtypeStruct((patches, fields, members, columns), F32),
+        scratch_shapes=[
+            pltpu.VMEM((patches, fields, members, columns), BF16),
+            pltpu.VMEM((patches, fields, members, columns), F32),
+            pltpu.SemaphoreType.DMA((patches,)),
+            pltpu.SemaphoreType.DMA((patches,)),
+        ],
         name="update",
     )(
         base,

time: 223 us -> 183 us (0.82)
  Pallas kernels: 190 us -> 149 us
    pallas_call x3, Pallas kernels: 71.6 us -> 37.7 us  [the longest x1 19.4 us: on_device(): pl.pallas_call(functools.partial(update_kernel, PAIR), in_specs=[smem, vm...]
    pallas_call x1, Pallas kernels: 74.5 us -> 67.9 us  [on_device(): pl.pallas_call(functools.partial(gram_kernel, per, lon_patches, lat_patch...]
where the time goes in v3:
time: 183 us; the launch traced here: 182 us
  Pallas kernels  149 us (81%)
  starting transfers between devices  11.5 us (6%)
  waiting for transfers between devices  6.96 us (4%)
  other arithmetic  6.74 us (4%)
  local copies, waits for them, and re-layouts  5.81 us (3%)
  between operations  2.07 us (1%)
    pallas_call x1, Pallas kernels, on_device(): pl.pallas_call(functools.partial(gram_kernel, per, lon_patches, lat_patch...  67.9 us
    pallas_call x1, Pallas kernels, on_device(): pl.pallas_call(plane_kernel, in_specs=[pl.BlockSpec(memory_space=pl.ANY)]...  43.7 us
    pallas_call x1, Pallas kernels, on_device(): pl.pallas_call(functools.partial(update_kernel, PAIR), in_specs=[smem, vm...  19.4 us
    pallas_call x1, Pallas kernels, on_device(): pl.pallas_call(functools.partial(add_kernel, per), in_specs=[smem, smem,...  13.6 us
    all_to_all x1, starting transfers between devices, on_device(): lax.all_to_all(message, AXES, split_axis=0, concat_axis=0, tiled=True)  11.5 us
    all_to_all x1, waiting for transfers between devices, on_device(): lax.all_to_all(message, AXES, split_axis=0, concat_axis=0, tiled=True)  6.96 us
    pallas_call x1, Pallas kernels, on_device(): pl.pallas_call(functools.partial(totals_kernel, turn), in_specs=[anywhere...  4.76 us
  transfers between devices with their start and end apart: 1, of which 1 were waited for; matrix products, arithmetic and copies ran while one was open for 1% of the time, Pallas kernels for 0%

profile of v3, /device:TPU:1, one launch (start us, length us, event | category | flops | bytes accessed | tf_op | source)
XLA Modules:
  0.0 182.4 jit_solution(14509239324552941336)
XLA Ops:
  0.0 0.7 broadcast_divide_fusion
  0.7 0.7 sign_compare_fusion
  1.4 0.1 div.73
  1.5 0.1 ne.117
  1.6 0.1 rem.95
  1.7 0.8 copy.21
  2.4 0.1 reshape.163
  2.6 0.1 reshape.164
  2.7 0.4 convert_reduce_fusion
  3.1 0.3 select_reduce_fusion
  3.4 0.1 convert_element_type.34
  3.6 4.8 %totals.1 = (f32[16,128]{1,0:T(8,128)}, bf16[192,16,128]{2,1,0:T(8,128)(2,1)}) custom-call(bf16[192,128,128]{2,1,0:T(8,128)(2,1)} %anom_ref.3, f32[192,128]{1,0:T(8,128)} %rinv_ref.3, f32[192,128]{1,0:T(8,128)} %innov_ref.1), custom_call_target="tpu_custom_call" | custom-call | tf_op jit(solution)/shard_map/totals/pallas_call | solution.py:419
  8.3 1.3 slice_reduce_fusion.2
  10.3 0.6 pad_maximum_fusion.1
  10.9 0.6 pad_maximum_fusion
  11.6 11.5 %all-to-all-start = ((f32[128,1,8]{2,1,0:T(1,128)}), f32[128,1,8]{2,1,0:T(1,128)S(1)}, u32[]{:S(2)}, u32[]{:S(2)}) async-start(f32[128,1,8]{2,1,0:T(1,128)} %bitcast.3), calls=%async_computation | async-start | bytes 131072 | tf_op jit(solution)/shard_map/all_to_all | solution.py:454
  23.1 0.6 pad_add_fusion.me_ref
  23.7 0.6 convert_element_type.37.lon_ref
  24.3 0.7 convert_element_type.38.lat_ref
  25.0 0.7 copy.26
  25.6 7.0 %all-to-all-done = f32[128,1,8]{2,1,0:T(1,128)S(1)} async-done(((f32[128,1,8]{2,1,0:T(1,128)}), f32[128,1,8]{2,1,0:T(1,128)S(1)}, u32[]{:S(2)}, u32[]{:S(2)}) %all-to-all-start) | async-done | bytes 4128 | tf_op jit(solution)/shard_map/all_to_all | solution.py:454
  32.7 0.1 slice_reduce_fusion
  32.8 0.6 fusion.19
  33.4 0.1 copy.24
  33.5 0.7 convert_element_type.36.code_ref
  34.2 0.1 copy.25
  34.3 0.7 reshape.171.table_ref
  35.0 67.9 %grams.1 = (bf16[3,8,16,144,128]{4,3,2,1,0:T(8,128)(2,1)}, s32[3,8,8,128]{3,2,1,0:T(8,128)}) custom-call(s32[1024]{0:T(1024)} %convert_element_type.36.code_ref, s32[8,128]{1,0:T(8,128)} %reshape.171.table_ref, bf16[192,128,128]{2,1,0:T(8,128)(2,1)} %anom_ref.3, bf16[192,16,128]{2,1,0:T(8,128)(2,1)} %get-tuple-element.10.ext_ref, f32[192,128]{1,0:T(8,128)} %rinv_ref.3, ...), custom_call_target="tpu_custom_call" | custom-call | tf_op jit(solution)/shard_map/grams/pallas_call | solution.py:462
  102.8 1.5 reshape.165.starts_ref
  104.4 13.6 %adds.1.dense_ref = bf16[3,16,384,128]{3,2,1,0:T(8,128)(2,1)} custom-call(s32[4]{0:T(128)} %pad_add_fusion.me_ref, s32[3,8,1024]{2,1,0:T(8,128)} %reshape.165.starts_ref, bf16[3,8,16,144,128]{4,3,2,1,0:T(8,128)(2,1)} %get-tuple-element.12.got_ref), custom_call_target="tpu_custom_call" | custom-call | tf_op jit(solution)/shard_map/adds/pallas_call | solution.py:485
  118.0 43.7 %planes.1.acc_ref = f32[16,72,128]{2,1,0:T(8,128)} custom-call(bf16[3,16,384,128]{3,2,1,0:T(8,128)(2,1)} %adds.1.dense_ref), custom_call_target="tpu_custom_call" | custom-call | tf_op jit(solution)/shard_map/planes/pallas_call | solution.py:500
  163.0 19.4 %update.1 = f32[16,6,128,256]{3,2,1,0:T(8,128)} custom-call(f32[1]{0:T(128)S(6)} %div.79.base_ref, f32[16,72,128]{2,1,0:T(8,128)} %planes.1.acc_ref, bf16[16,6,128,256]{3,2,1,0:T(8,128)(2,1)} %bitcast.19, f32[16,6,256]{2,1,0:T(8,128)} %bitcast.21), custom_call_target="tpu_custom_call" | custom-call | tf_op jit(solution)/shard_map/update/pallas_call | solution.py:515
  (13 shorter events, 0.2 us)
Async XLA Ops:
  3.5 20.2 %copy-start.1 = (s32[192,128]{1,0:T(8,128)S(1)}, s32[192,128]{1,0:T(8,128)}, u32[]{:S(2)}) copy-start(s32[192,128]{1,0:T(8,128)} %param.14) | copy-start | bytes 294916
  3.5 20.8 %copy-start.2 = (s32[192,128]{1,0:T(8,128)S(1)}, s32[192,128]{1,0:T(8,128)}, u32[]{:S(2)}) copy-start(s32[192,128]{1,0:T(8,128)} %param.15) | copy-start | bytes 294916
  3.6 21.4 %copy-start = (f32[8,2,6,256]{3,1,2,0:T(2,128)S(1)}, f32[8,2,6,256]{3,1,2,0:T(2,128)}, u32[]{:S(2)}) copy-start(f32[8,2,6,256]{3,1,2,0:T(2,128)} %param.10) | copy-start | bytes 294916
  11.6 21.1 %all-to-all-start = ((f32[128,1,8]{2,1,0:T(1,128)}), f32[128,1,8]{2,1,0:T(1,128)S(1)}, u32[]{:S(2)}, u32[]{:S(2)}) async-start(f32[128,1,8]{2,1,0:T(1,128)} %bitcast.3), calls=%async_computation | async-start | bytes 131072 | tf_op jit(solution)/shard_map/all_to_all | solution.py:454

commit v4 on v3

--- a/solution.py
+++ b/solution.py
@@ -18,39 +18,84 @@
 BF16 = jnp.bfloat16
 
 
-def totals_kernel(turn, anom_ref, rinv_ref, innov_ref, out_ref, ext_ref, held, sems):
+def request_kernel(turn, members_less, anom_ref, rinv_ref, innov_ref, ask_ref, got_ref, ext_ref, held, row_out, row_in,
+                   sems, send, recv):
     blocks, _, width = anom_ref.shape
     turns = blocks // turn
+    holders = ask_ref.shape[0]
+    lat_devices = lax.axis_size("lat")
+    me = lax.axis_index("lon") * lat_devices + lax.axis_index("lat")
 
     def copy(k):
         return pltpu.make_async_copy(
             anom_ref.at[pl.ds(k * turn, turn)], held.at[pl.ds(k * turn, turn)], sems.at[k]
         )
 
+    def to_holder(step):
+        other = lax.rem(me + step, holders)
+        device = (lax.div(other, lat_devices), lax.rem(other, lat_devices))
+        return other, device
+
     for k in range(turns):
         copy(k).start()
+    barrier = pltpu.get_barrier_semaphore()
+
+    def signal(step, carry):
+        _, device = to_holder(step)
+        pl.semaphore_signal(barrier, inc=1, device_id=device, device_id_type=MESH)
+        return carry
+
+    lax.fori_loop(1, holders, signal, 0)
+
     innov = innov_ref[...]
+    first = jnp.sum((rinv_ref[...] * innov * innov).reshape(blocks // 8, 8, width), axis=0)
+
+    def one(k, total):
+        copy(k).wait()
+        start = pl.multiple_of(k * turn, turn)
+        rinv = rinv_ref[pl.ds(start, turn), :]
+        for b in range(turn):
+            a = held[start + b].astype(F32)
+            squares = jnp.sum((a * a).reshape(-1, 8, width), axis=0)
+            total = total + squares * rinv[b : b + 1, :]
+        return total
+
+    second = lax.fori_loop(0, turns, one, jnp.zeros((8, width), F32))
+
+    def whole(x):
+        return jnp.sum(jnp.sum(x, axis=0, keepdims=True), axis=1, keepdims=True)
+
+    lane = lax.broadcasted_iota(jnp.int32, (1, width), 1)
+    sums = jnp.where(lane == 6, whole(first), 0.0) + jnp.where(lane == 7, whole(second) / members_less, 0.0)
+    rows = ask_ref[...] + sums[None]
+    row_out[...] = rows
     high = innov.astype(BF16).astype(F32)
     rest = innov - high
     mid = rest.astype(BF16).astype(F32)
-    low = rest - mid
     ext = jnp.concatenate(
-        [high[:, None, :], mid[:, None, :], low[:, None, :], jnp.zeros((blocks, 13, width), F32)], axis=1
+        [high[:, None, :], mid[:, None, :], (rest - mid)[:, None, :], jnp.zeros((blocks, 13, width), F32)],
+        axis=1,
     )
     ext_ref[...] = ext.astype(BF16)
-    out_ref[0:8, :] = jnp.sum((rinv_ref[...] * innov * innov).reshape(blocks // 8, 8, width), axis=0)
-
-    def one(k, total):
-        copy(k).wait()
-        first = pl.multiple_of(k * turn, turn)
-        rinv = rinv_ref[pl.ds(first, turn), :]
-        for b in range(turn):
-            a = held[first + b].astype(F32)
-            squares = jnp.sum((a * a).reshape(-1, 8, width), axis=0)
-            total = total + squares * rinv[b : b + 1, :]
-        return total
-
-    out_ref[8:16, :] = lax.fori_loop(0, turns, one, jnp.zeros((8, width), F32))
+    pl.semaphore_wait(barrier, holders - 1)
+
+    def ask(step, carry):
+        other, device = to_holder(step)
+        pltpu.make_async_remote_copy(
+            src_ref=row_out.at[other],
+            dst_ref=row_in.at[me],
+            send_sem=send,
+            recv_sem=recv,
+            device_id=device,
+            device_id_type=MESH,
+        ).start()
+        return carry
+
+    lax.fori_loop(1, holders, ask, 0)
+    units_wait(row_out.at[0 : holders - 1], send)
+    units_wait(row_in.at[0 : holders - 1], recv)
+    got_ref[...] = row_in[...]
+    got_ref[me] = row_out[me]
 
 
 def coordinates():
@@ -177,9 +222,9 @@
             held = code >> 8
             cl = (lon_first + (code & 112)).astype(F32) + (PSIDE - 1) / 2.0
             ct = (lat_first + ((code & 128) >> 3)).astype(F32) + (PSIDE - 1) / 2.0
-            gap = jnp.abs(lon_ref[pl.ds(held, 1), :] - cl)
+            gap = jnp.abs(lon_ref[pl.ds(held, 1), :].astype(F32) - cl)
             gap = jnp.minimum(gap, grid_lon - gap)
-            other = lat_ref[pl.ds(held, 1), :] - ct
+            other = lat_ref[pl.ds(held, 1), :].astype(F32) - ct
             weight = rinv_ref[pl.ds(held, 1), :] * jnp.exp(
                 -(gap * gap + other * other) / (2.0 * LOC_SCALE * LOC_SCALE)
             )
@@ -253,7 +298,7 @@
                 for s in range(0, per, 2):
                     both = held[q, source, place, s * third : (s + 2) * third, :].astype(F32)
                     for t in range(2):
-                        start = pl.multiple_of(starts_ref[q, source, first + s + t], 8)
+                        start = pl.multiple_of(starts_ref[first + ((q * sources + source) * 1024 + s + t)], 8)
                         accs[(s + t) % chains][pl.ds(start, third), :] += both[t * third : (t + 1) * third]
             if q < 2:
                 made[q, place] = functools.reduce(lambda a, b: a + b, [acc[...] for acc in accs]).astype(BF16)
@@ -415,24 +460,6 @@
     vmem = pl.BlockSpec(memory_space=pltpu.VMEM)
     smem = pl.BlockSpec(memory_space=pltpu.SMEM)
     anywhere = pl.BlockSpec(memory_space=pl.ANY)
-    turn = 16
-    sums, ext = pl.pallas_call(
-        functools.partial(totals_kernel, turn),
-        in_specs=[anywhere, vmem, vmem],
-        out_specs=[vmem, vmem],
-        out_shape=[
-            jax.ShapeDtypeStruct((16, block_obs), F32),
-            jax.ShapeDtypeStruct((held_blocks, 16, block_obs), BF16),
-        ],
-        scratch_shapes=[
-            pltpu.VMEM((held_blocks, members, block_obs), BF16),
-            pltpu.SemaphoreType.DMA((held_blocks // turn,)),
-        ],
-        name="totals",
-    )(obs_anom, obs_rinv, innov)
-    first_sum = jnp.sum(sums[0:8])
-    second_sum = jnp.sum(sums[8:16]) / (members - 1)
-
     wanted = block_list.reshape(slots)
     holder = wanted // held_blocks
     slot = jnp.arange(slots)
@@ -444,14 +471,28 @@
     rank = jnp.sum(earlier.astype(jnp.int32), axis=1)
     bucket = holder * per + rank
     requests = jnp.sum(jnp.where(bucket[:, None] == slot[None, :], code[:, None], 0), axis=0)
-    message = jnp.concatenate(
-        [
-            requests.reshape(holders, per).astype(F32),
-            jnp.broadcast_to(jnp.stack([first_sum, second_sum])[None, :], (holders, 2)),
+    message = jnp.pad(requests.reshape(holders, 1, per).astype(F32), ((0, 0), (0, 0), (0, block_obs - per)))
+    turn = 16
+    asked, ext = pl.pallas_call(
+        functools.partial(request_kernel, turn, float(members - 1)),
+        in_specs=[anywhere, vmem, vmem, vmem],
+        out_specs=[vmem, vmem],
+        out_shape=[
+            jax.ShapeDtypeStruct((holders, 1, block_obs), F32),
+            jax.ShapeDtypeStruct((held_blocks, 16, block_obs), BF16),
         ],
-        axis=1,
-    )
-    asked = lax.all_to_all(message, AXES, split_axis=0, concat_axis=0, tiled=True)
+        scratch_shapes=[
+            pltpu.VMEM((held_blocks, members, block_obs), BF16),
+            pltpu.VMEM((holders, 1, block_obs), F32),
+            pltpu.VMEM((holders, 1, block_obs), F32),
+            pltpu.SemaphoreType.DMA((held_blocks // turn,)),
+            pltpu.SemaphoreType.DMA,
+            pltpu.SemaphoreType.DMA,
+        ],
+        compiler_params=pltpu.CompilerParams(collective_id=2, has_side_effects=True),
+        name="requests",
+    )(obs_anom, obs_rinv, innov, message)
+    asked = asked.reshape(holders, block_obs)[:, :8]
     total = jnp.sum(asked[:, per:], axis=0)
     inflation = total[0] / (total[1] + holders * held_blocks * block_obs)
     base = ((members - 1) / inflation).reshape(1)
@@ -479,7 +520,7 @@
         ],
         compiler_params=pltpu.CompilerParams(collective_id=0, has_side_effects=True),
         name="grams",
-    )(codes, starts.reshape(8, 128), obs_anom, ext, obs_rinv, obs_lon.astype(F32), obs_lat.astype(F32))
+    )(codes, starts.reshape(8, 128), obs_anom, ext, obs_rinv, obs_lon, obs_lat)
 
     x, y, z, core = coordinates()
     dense = pl.pallas_call(
@@ -495,7 +536,7 @@
         ]
         + [pltpu.VMEM((patches * third, members), F32)] * CHAINS,
         name="adds",
-    )(jnp.stack([x, y, z, core]), tables.reshape(3, 8, 1024), got)
+    )(jnp.stack([x, y, z, core]), tables.reshape(3 * 8 * 1024), got)
 
     acc = pl.pallas_call(
         plane_kernel,

time: 183 us -> 177 us (0.967)
  Pallas kernels: 149 us -> 165 us
  starting transfers between devices: 11.5 us -> 0 us
  waiting for transfers between devices: 6.96 us -> 0 us
    pallas_call x1, Pallas kernels: 4.76 us -> 18.3 us  [on_device(): pl.pallas_call(functools.partial(request_kernel, turn, float(members - 1)...]
    all_to_all x1 -> x0, starting transfers between devices: 11.5 us -> none  [on_device(): lax.all_to_all(message, AXES, split_axis=0, concat_axis=0, tiled=True)]
    all_to_all x1 -> x0, waiting for transfers between devices: 6.96 us -> none  [on_device(): lax.all_to_all(message, AXES, split_axis=0, concat_axis=0, tiled=True)]
  transfers between devices with their start and end apart: 1 -> 0, of which waited for: 1 -> 0; matrix products, arithmetic and copies ran while one was open for 1% -> 0% of each run, Pallas kernels for 0% -> 0%
where the time goes in v4:
time: 177 us
  Pallas kernels  165 us (93%)
  other arithmetic  5.35 us (3%)
  local copies, waits for them, and re-layouts  4.68 us (3%)
    pallas_call x1, Pallas kernels, on_device(): pl.pallas_call(functools.partial(gram_kernel, per, lon_patches, lat_patch...  67.9 us
    pallas_call x1, Pallas kernels, on_device(): pl.pallas_call(plane_kernel, in_specs=[pl.BlockSpec(memory_space=pl.ANY)]...  45.2 us
    pallas_call x1, Pallas kernels, on_device(): pl.pallas_call(functools.partial(update_kernel, PAIR), in_specs=[smem, vm...  19.4 us
    pallas_call x1, Pallas kernels, on_device(): pl.pallas_call(functools.partial(request_kernel, turn, float(members - 1)...  18.3 us
    pallas_call x1, Pallas kernels, on_device(): pl.pallas_call(functools.partial(add_kernel, per), in_specs=[smem, smem,...  14.4 us

profile of v4, /device:TPU:1, one launch (start us, length us, event | category | flops | bytes accessed | tf_op | source)
XLA Modules:
  0.0 176.8 jit_solution(13409396496297431276)
XLA Ops:
  0.0 0.7 broadcast_divide_fusion
  0.7 0.1 div.70
  0.8 0.7 sign_compare_fusion
  1.5 0.1 ne.117
  1.6 0.1 rem.95
  1.7 0.8 copy.18
  2.4 0.1 reshape.175
  2.5 0.1 broadcast_in_dim.10
  2.6 0.1 reshape.176
  2.7 0.4 convert_reduce_fusion
  3.1 0.3 select_reduce_fusion
  3.4 0.1 convert_element_type.32
  3.5 0.7 pad.4.ask_ref
  4.2 18.3 %requests.1 = (f32[128,1,128]{2,1,0:T(1,128)}, bf16[192,16,128]{2,1,0:T(8,128)(2,1)}) custom-call(bf16[192,128,128]{2,1,0:T(8,128)(2,1)} %anom_ref.3, f32[192,128]{1,0:T(8,128)} %rinv_ref.3, f32[192,128]{1,0:T(8,128)} %innov_ref.1, f32[128,1,128]{2,1,0:T(1,128)} %pad.4.ask_ref), custom_call_target="tpu_custom_call" | custom-call | tf_op jit(solution)/shard_map/requests/pallas_call | solution.py:476
  22.5 0.9 slice_reduce_fusion
  23.4 0.6 fusion.19
  25.4 0.6 pad_add_fusion.me_ref
  26.0 0.8 slice_convert_fusion
  26.8 0.7 reshape.178.code_ref
  27.5 0.9 add_multiply_fusion
  28.4 0.7 reshape.184.table_ref
  29.0 67.9 %grams.1 = (bf16[3,8,16,144,128]{4,3,2,1,0:T(8,128)(2,1)}, s32[3,8,8,128]{3,2,1,0:T(8,128)}) custom-call(s32[1024]{0:T(1024)} %reshape.178.code_ref, s32[8,128]{1,0:T(8,128)} %reshape.184.table_ref, bf16[192,128,128]{2,1,0:T(8,128)(2,1)} %anom_ref.3, bf16[192,16,128]{2,1,0:T(8,128)(2,1)} %get-tuple-element.10.ext_ref, f32[192,128]{1,0:T(8,128)} %rinv_ref.3, ...), custom_call_target="tpu_custom_call" | custom-call | tf_op jit(solution)/shard_map/grams/pallas_call | solution.py:503
  97.0 14.4 %adds.1.dense_ref = bf16[3,16,384,128]{3,2,1,0:T(8,128)(2,1)} custom-call(s32[4]{0:T(128)} %pad_add_fusion.me_ref, s32[24576]{0:T(1024)} %bitcast.16, bf16[3,8,16,144,128]{4,3,2,1,0:T(8,128)(2,1)} %get-tuple-element.12.got_ref), custom_call_target="tpu_custom_call" | custom-call | tf_op jit(solution)/shard_map/adds/pallas_call | solution.py:526
  111.4 0.0 copy-start
  111.5 45.2 %planes.1.acc_ref = f32[16,72,128]{2,1,0:T(8,128)} custom-call(bf16[3,16,384,128]{3,2,1,0:T(8,128)(2,1)} %adds.1.dense_ref), custom_call_target="tpu_custom_call" | custom-call | tf_op jit(solution)/shard_map/planes/pallas_call | solution.py:541
  156.7 0.0 copy-done
  156.7 0.7 copy.20
  157.3 19.4 %update.1 = f32[16,6,128,256]{3,2,1,0:T(8,128)} custom-call(f32[1]{0:T(128)S(6)} %div.75.base_ref, f32[16,72,128]{2,1,0:T(8,128)} %planes.1.acc_ref, bf16[16,6,128,256]{3,2,1,0:T(8,128)(2,1)} %bitcast.10, f32[16,6,256]{2,1,0:T(8,128)} %bitcast.14), custom_call_target="tpu_custom_call" | custom-call | tf_op jit(solution)/shard_map/update/pallas_call | solution.py:556
  (3 shorter events, 0.0 us)
Async XLA Ops:
  111.4 45.2 %copy-start = (f32[8,2,6,256]{3,1,2,0:T(2,128)S(1)}, f32[8,2,6,256]{3,1,2,0:T(2,128)}, u32[]{:S(2)}) copy-start(f32[8,2,6,256]{3,1,2,0:T(2,128)} %param.10) | copy-start | bytes 294916

commit v5 on v4

--- a/solution.py
+++ b/solution.py
@@ -18,7 +18,7 @@
 BF16 = jnp.bfloat16
 
 
-def request_kernel(turn, members_less, anom_ref, rinv_ref, innov_ref, ask_ref, got_ref, ext_ref, held, row_out, row_in,
+def request_kernel(turn, members_less, anom_ref, rinv_ref, innov_ref, ask_ref, got_ref, codes_ref, ext_ref, held, row_out, row_in,
                    sems, send, recv):
     blocks, _, width = anom_ref.shape
     turns = blocks // turn
@@ -96,6 +96,8 @@
     units_wait(row_in.at[0 : holders - 1], recv)
     got_ref[...] = row_in[...]
     got_ref[me] = row_out[me]
+    codes_ref[...] = row_in[...].astype(jnp.int32)
+    codes_ref[me] = row_out[me].astype(jnp.int32)
 
 
 def coordinates():
@@ -117,12 +119,8 @@
     for step in (1, 2, 3)
     for core in (0, 1)
 ]
-PLANE_PEERS = [
-    (dx, dy, dz, 0)
-    for dx in range(4)
-    for dy in range(4)
-    for dz in range(4)
-    if 0 < (dx != 0) + (dy != 0) + (dz != 0) < 3
+AXIS_PEERS = [
+    tuple(step if axis == a else 0 for a in range(3)) + (0,) for axis in range(3) for step in (1, 2, 3)
 ]
 
 
@@ -156,10 +154,12 @@
 
 
 def gram_kernel(per, lon_patches, lat_patches, code_ref, table_ref, anom_ref, ext_ref, rinv_ref,
-                lon_ref, lat_ref, got_ref, codes_ref, stage, send, recv, own, send2, recv2, own2):
+                lon_ref, lat_ref, got_ref, codes_ref, stage, blocks, block_sems, send, recv, own, send2, recv2, own2):
     me = coordinates()
     xm, ym, zm, cm = me
     mine = (zm, xm, ym)
+    chunks = block_sems.shape[0]
+    turn = anom_ref.shape[0] // chunks
     members = anom_ref.shape[1]
     half = members // 2
     third = (half + 8) // 3
@@ -171,6 +171,12 @@
     on_diag = row == lane
     row8 = lax.broadcasted_iota(jnp.int32, (8, members), 0)
 
+    def fetch(k):
+        part = pl.ds(k * turn, turn)
+        return pltpu.make_async_copy(anom_ref.at[part], blocks.at[part], block_sems.at[k])
+
+    for k in range(chunks):
+        fetch(k).start()
     greet(me, LINE_PEERS)
     for q in range(3):
         source = mine[q] * 2 + cm
@@ -184,6 +190,9 @@
                 else:
                     remote(table_ref, dst, send2, recv2, shifted(me, offset)).start()
 
+    for k in range(chunks):
+        fetch(k).wait()
+
     def offset_of(i):
         dx = lax.rem(i, 4)
         dy = lax.rem(i + lax.div(i, 4), 4)
@@ -194,7 +203,7 @@
         dx, dy, dz, dc = offset_of(i)
         x, y, z, core = shifted(me, (dx, dy, dz, dc))
         targets = ((xm, ym, z, core), (x, ym, zm, core), (xm, y, zm, core))
-        places = (x * 4 + y, y * 4 + z, x * 4 + z)
+        places = (x * 4 + y, y * 4 + z, z * 4 + x)
         for q, moved in enumerate((dz, dx, dy)):
             src = stage.at[i, q]
             dst = got_ref.at[q, mine[q] * 2 + cm, places[q]]
@@ -212,7 +221,7 @@
         x, y, z, core = shifted(me, offset_of(i))
         lon_device = y * 2 + core
         lat_device = x * 4 + z
-        who8 = (lon_device * 16 + lat_device) * 8
+        who8 = (lon_device * 16 + lat_device) * members
         lon_first = lon_device * (lon_patches * PSIDE)
         lat_first = lat_device * (lat_patches * PSIDE)
         pieces = []
@@ -229,7 +238,7 @@
                 -(gap * gap + other * other) / (2.0 * LOC_SCALE * LOC_SCALE)
             )
             weight = weight * valid.astype(F32)
-            a = anom_ref[held]
+            a = blocks[held]
             scaled = (a.astype(F32) * weight).astype(BF16)
             left = jnp.concatenate([a, ext_ref[held]], axis=0)
             full = lax.dot_general(
@@ -270,11 +279,23 @@
     units_wait(got_ref.at[:, 0:7], recv)
 
 
-def add_kernel(per, me_ref, starts_ref, got_ref, out_ref, held, made, sems, out_sems, *accs):
+def split_again(total, third):
+    row8 = lax.broadcasted_iota(jnp.int32, (8, total.shape[1]), 0)
+    parts = []
+    for t in range(2):
+        top = total[t * third : t * third + 16]
+        last = total[t * third + 16 : (t + 1) * third]
+        proj = last[1:2, :] + last[2:3, :]
+        high = proj.astype(BF16).astype(F32)
+        parts += [top, jnp.where(row8 == 1, high, jnp.where(row8 == 2, proj - high, last))]
+    return jnp.concatenate(parts, axis=0)
+
+
+def add_kernel(per, starts_ref, got_ref, out_ref, held, made, sems, out_sems, *accs):
     sources, places = held.shape[1:3]
     third = held.shape[3] // per
     chains = len(accs)
-    row8 = lax.broadcasted_iota(jnp.int32, (8, held.shape[4]), 0)
+    xm, ym, zm, cm = coordinates()
 
     def copy(q, source):
         return pltpu.make_async_copy(got_ref.at[q, source], held.at[q, source], sems.at[q, source])
@@ -288,10 +309,10 @@
 
         def one(place, carry):
             major, minor = lax.div(place, 4), lax.rem(place, 4)
-            x = me_ref[0] if q == 1 else major
-            y = me_ref[1] if q == 2 else (minor if q == 0 else major)
-            z = me_ref[2] if q == 0 else minor
-            first = ((y * 2 + me_ref[3]) * 16 + x * 4 + z) * 8
+            x = (major, xm, minor)[q]
+            y = (minor, major, ym)[q]
+            z = (zm, minor, major)[q]
+            first = ((y * 2 + cm) * 16 + x * 4 + z) * 8
             for acc in accs:
                 acc[...] = jnp.zeros_like(acc)
             for source in range(sources):
@@ -306,14 +327,7 @@
                 for p in range(0, accs[0].shape[0] // third, 2):
                     rows = slice(p * third, (p + 2) * third)
                     total = functools.reduce(lambda a, b: a + b, [acc[rows, :] for acc in accs])
-                    parts = []
-                    for t in range(2):
-                        top = total[t * third : t * third + 16]
-                        last = total[t * third + 16 : (t + 1) * third]
-                        proj = last[1:2, :] + last[2:3, :]
-                        high = proj.astype(BF16).astype(F32)
-                        parts += [top, jnp.where(row8 == 1, high, jnp.where(row8 == 2, proj - high, last))]
-                    made[q, place, rows, :] = jnp.concatenate(parts, axis=0).astype(BF16)
+                    made[q, place, rows, :] = split_again(total, third).astype(BF16)
             return carry
 
         lax.fori_loop(0, places, one, 0)
@@ -322,39 +336,64 @@
         pltpu.make_async_copy(made.at[q], out_ref.at[q], out_sems.at[q]).wait()
 
 
-def plane_kernel(dense_ref, acc_ref, held, send, recv, own):
+def plane_kernel(dense_ref, acc_ref, held, mids, lasts, send, recv, send2, recv2, own):
     me = coordinates()
-    xm, ym, zm, cm = me
-    places = (xm * 4 + ym, ym * 4 + zm, xm * 4 + zm)
-    third = dense_ref.shape[2] // acc_ref.shape[0]
-    greet(me, PLANE_PEERS)
-    for k in range(16):
-        first, second = k % 4, (k + k // 4) % 4
+    xm, ym, zm, _ = me
+    firsts, seconds = (xm, ym, zm), (ym, zm, xm)
+    rows = dense_ref.shape[2]
+    third = rows // acc_ref.shape[0]
+
+    def along(axis, step):
+        return shifted(me, tuple(step if a == axis else 0 for a in range(3)) + (0,))
+
+    greet(me, AXIS_PEERS)
+    for q in range(3):
+        mine = dense_ref.at[q, pl.ds(firsts[q] * 4, 4)]
+        pltpu.make_async_copy(mine, held.at[q, firsts[q]], own.at[q]).start()
+    for step in (2, 1, 3):
         for q in range(3):
-            offset = ((first, second, 0, 0), (0, first, second, 0), (first, 0, second, 0))[q]
-            x, y, z, core = shifted(me, offset)
-            place = (x * 4 + y, y * 4 + z, x * 4 + z)[q]
-            src = dense_ref.at[q, place]
-            dst = held.at[q, places[q]]
-            if first == 0 and second == 0:
-                pltpu.make_async_copy(src, dst, own.at[q]).start()
-            else:
-                remote(src, dst, send, recv.at[q], (x, y, z, core)).start()
-    for q in range(3):
-        pltpu.make_async_copy(dense_ref.at[q, 0], held.at[q, 0], own.at[q]).wait()
-        units_wait(held.at[q, 0:15], recv.at[q])
-
-        def one(j, carry):
+            other = lax.rem(firsts[q] + step, 4)
+            remote(
+                dense_ref.at[q, pl.ds(other * 4, 4)], held.at[q, firsts[q]], send, recv.at[q],
+                along(q, step),
+            ).start()
+    for q in range(3):
+        pltpu.make_async_copy(dense_ref.at[q, 0:4], held.at[q, 0], own.at[q]).wait()
+        units_wait(held.at[q, 0:3], recv.at[q])
+
+        def one(k, carry):
+            place = lax.rem(seconds[q] + 1 + lax.div(k, rows // (2 * third)), 4)
+            start = pl.multiple_of(lax.rem(k, rows // (2 * third)) * (2 * third), 16)
+            total = held[q, 0, place, pl.ds(start, 2 * third), :].astype(F32)
+            for source in range(1, 4):
+                total += held[q, source, place, pl.ds(start, 2 * third), :].astype(F32)
+            if q == 2:
+                total = split_again(total, third)
+            mids[q, place, pl.ds(start, 2 * third), :] = total.astype(BF16)
+            return carry
+
+        lax.fori_loop(0, 4 * rows // (2 * third), one, 0)
+        for step in (2, 1, 3):
+            other = lax.rem(seconds[q] + step, 4)
+            remote(
+                mids.at[q, other], lasts.at[q, seconds[q]], send2, recv2.at[q], along((q + 1) % 3, step)
+            ).start()
+        lasts[q, seconds[q]] = mids[q, seconds[q]]
+    for q in range(3):
+        units_wait(lasts.at[q, 0:3], recv2.at[q])
+
+        def two(j, carry):
             start = pl.multiple_of(j * 2 * third, 16)
-            total = held[q, 0, pl.ds(start, 2 * third), :].astype(F32)
-            for source in range(1, 16):
-                total += held[q, source, pl.ds(start, 2 * third), :].astype(F32)
+            total = lasts[q, 0, pl.ds(start, 2 * third), :].astype(F32)
+            for source in range(1, 4):
+                total += lasts[q, source, pl.ds(start, 2 * third), :].astype(F32)
             acc_ref[2 * j, q * third : (q + 1) * third, :] = total[:third]
             acc_ref[2 * j + 1, q * third : (q + 1) * third, :] = total[third:]
             return carry
 
-        lax.fori_loop(0, acc_ref.shape[0] // 2, one, 0)
-    units_wait(held.at[:, 0:15], send)
+        lax.fori_loop(0, acc_ref.shape[0] // 2, two, 0)
+    units_wait(held.at[:, 0:3], send)
+    units_wait(lasts.at[:, 0:3], send2)
 
 
 def halves(x):
@@ -378,7 +417,7 @@
     return found
 
 
-def update_kernel(count, base_ref, acc_ref, pert_ref, mean_ref, out_ref, perts, made, sems, out_sems):
+def update_kernel(count, observations, asked_ref, acc_ref, pert_ref, mean_ref, out_ref, perts, made, sems, out_sems):
     patches, fields, members, _ = pert_ref.shape
 
     def take(p):
@@ -389,9 +428,10 @@
 
     for p in range(patches):
         take(p).start()
+    base = float(members - 1) / base_of(asked_ref, observations)
 
     def one(g, carry):
-        update_patches(g * count, count, fields, members, base_ref, acc_ref, mean_ref, perts, made, take, put)
+        update_patches(g * count, count, fields, members, base, acc_ref, mean_ref, perts, made, take, put)
         return carry
 
     lax.fori_loop(0, patches // count, one, 0)
@@ -399,14 +439,21 @@
         put(p).wait()
 
 
-def update_patches(first, count, fields, members, base_ref, acc_ref, mean_ref, perts, made, take, put):
+def base_of(asked_ref, observations):
+    total = jnp.sum(asked_ref[...], axis=0)
+    lane = lax.broadcasted_iota(jnp.int32, total.shape, 1)
+    first = jnp.sum(jnp.where(lane == 6, total, 0.0), axis=1, keepdims=True)
+    second = jnp.sum(jnp.where(lane == 7, total, 0.0), axis=1, keepdims=True)
+    return first / (second + float(observations))
+
+
+def update_patches(first, count, fields, members, base, acc_ref, mean_ref, perts, made, take, put):
     half = members // 2
     row = lax.broadcasted_iota(jnp.int32, (members, members), 0)
     lane = lax.broadcasted_iota(jnp.int32, (members, members), 1)
     eye = jnp.where(row == lane, 1.0, 0.0)
     r = row[:half]
     c = lane[:half]
-    base = base_ref[0]
     state = []
     for q in range(count):
         packed = acc_ref[first + q, 0:half, :]
@@ -473,12 +520,13 @@
     requests = jnp.sum(jnp.where(bucket[:, None] == slot[None, :], code[:, None], 0), axis=0)
     message = jnp.pad(requests.reshape(holders, 1, per).astype(F32), ((0, 0), (0, 0), (0, block_obs - per)))
     turn = 16
-    asked, ext = pl.pallas_call(
+    asked, codes, ext = pl.pallas_call(
         functools.partial(request_kernel, turn, float(members - 1)),
         in_specs=[anywhere, vmem, vmem, vmem],
-        out_specs=[vmem, vmem],
+        out_specs=[vmem, vmem, vmem],
         out_shape=[
             jax.ShapeDtypeStruct((holders, 1, block_obs), F32),
+            jax.ShapeDtypeStruct((holders, 1, block_obs), jnp.int32),
             jax.ShapeDtypeStruct((held_blocks, 16, block_obs), BF16),
         ],
         scratch_shapes=[
@@ -492,18 +540,12 @@
         compiler_params=pltpu.CompilerParams(collective_id=2, has_side_effects=True),
         name="requests",
     )(obs_anom, obs_rinv, innov, message)
-    asked = asked.reshape(holders, block_obs)[:, :8]
-    total = jnp.sum(asked[:, per:], axis=0)
-    inflation = total[0] / (total[1] + holders * held_blocks * block_obs)
-    base = ((members - 1) / inflation).reshape(1)
-    codes = asked.astype(jnp.int32).reshape(holders * 8)
-
     third = (half + 8) // 3
-    starts = (((codes >> 4) & 7) * lat_patches + ((codes >> 7) & 1)) * third
+    short = codes.reshape(holders, block_obs)[:, :8].reshape(holders * 8)
+    starts = (((short >> 4) & 7) * lat_patches + ((short >> 7) & 1)) * third
     got, tables = pl.pallas_call(
         functools.partial(gram_kernel, per, lon_patches, lat_patches),
-        in_specs=[pl.BlockSpec(memory_space=pltpu.SMEM), pl.BlockSpec(memory_space=pl.ANY)]
-        + [pl.BlockSpec(memory_space=pltpu.VMEM)] * 5,
+        in_specs=[smem, anywhere, anywhere, vmem, vmem, vmem, vmem],
         out_specs=[pl.BlockSpec(memory_space=pl.ANY)] * 2,
         out_shape=[
             jax.ShapeDtypeStruct((3, 8, 16, per * third, members), BF16),
@@ -511,6 +553,8 @@
         ],
         scratch_shapes=[
             pltpu.VMEM((holders, 3, per * third, members), BF16),
+            pltpu.VMEM((held_blocks, members, block_obs), BF16),
+            pltpu.SemaphoreType.DMA((held_blocks // turn,)),
             pltpu.SemaphoreType.DMA,
             pltpu.SemaphoreType.DMA,
             pltpu.SemaphoreType.DMA,
@@ -520,12 +564,11 @@
         ],
         compiler_params=pltpu.CompilerParams(collective_id=0, has_side_effects=True),
         name="grams",
-    )(codes, starts.reshape(8, 128), obs_anom, ext, obs_rinv, obs_lon, obs_lat)
-
-    x, y, z, core = coordinates()
+    )(codes.reshape(holders * block_obs), starts.reshape(8, 128), obs_anom, ext, obs_rinv, obs_lon, obs_lat)
+
     dense = pl.pallas_call(
         functools.partial(add_kernel, per),
-        in_specs=[smem, smem, anywhere],
+        in_specs=[smem, anywhere],
         out_specs=anywhere,
         out_shape=jax.ShapeDtypeStruct((3, 16, patches * third, members), BF16),
         scratch_shapes=[
@@ -536,7 +579,7 @@
         ]
         + [pltpu.VMEM((patches * third, members), F32)] * CHAINS,
         name="adds",
-    )(jnp.stack([x, y, z, core]), tables.reshape(3 * 8 * 1024), got)
+    )(tables.reshape(3 * 8 * 1024), got)
 
     acc = pl.pallas_call(
         plane_kernel,
@@ -544,7 +587,11 @@
         out_specs=pl.BlockSpec(memory_space=pltpu.VMEM),
         out_shape=jax.ShapeDtypeStruct((patches, half + 8, members), F32),
         scratch_shapes=[
-            pltpu.VMEM((3, 16, patches * third, members), BF16),
+            pltpu.VMEM((3, 4, 4, patches * third, members), BF16),
+            pltpu.VMEM((3, 4, patches * third, members), BF16),
+            pltpu.VMEM((3, 4, patches * third, members), BF16),
+            pltpu.SemaphoreType.DMA,
+            pltpu.SemaphoreType.DMA((3,)),
             pltpu.SemaphoreType.DMA,
             pltpu.SemaphoreType.DMA((3,)),
             pltpu.SemaphoreType.DMA((3,)),
@@ -554,8 +601,8 @@
     )(dense)
 
     updated = pl.pallas_call(
-        functools.partial(update_kernel, PAIR),
-        in_specs=[smem, vmem, anywhere, vmem],
+        functools.partial(update_kernel, PAIR, holders * held_blocks * block_obs),
+        in_specs=[vmem, vmem, anywhere, vmem],
         out_specs=anywhere,
         out_shape=jax.ShapeDtypeStruct((patches, fields, members, columns), F32),
         scratch_shapes=[
@@ -566,7 +613,7 @@
         ],
         name="update",
     )(
-        base,
+        asked,
         acc,
         state_pert.reshape(patches, fields, members, columns),
         state_mean.reshape(patches, fields, columns),

time: 177 us -> 157 us (0.89)
  Pallas kernels: 165 us -> 150 us
  other arithmetic: 5.35 us -> 2.98 us
    pallas_call x1, Pallas kernels: 45.2 us -> 31.1 us  [on_device(): pl.pallas_call(plane_kernel, in_specs=[pl.BlockSpec(memory_space=pl.ANY)]...]
where the time goes in v5:
time: 157 us; the launch traced here: 156 us
  Pallas kernels  150 us (96%)
  local copies, waits for them, and re-layouts  3.39 us (2%)
  other arithmetic  2.98 us (2%)
    pallas_call x1, Pallas kernels, on_device(): pl.pallas_call(functools.partial(gram_kernel, per, lon_patches, lat_patch...  66.8 us
    pallas_call x1, Pallas kernels, on_device(): pl.pallas_call(plane_kernel, in_specs=[pl.BlockSpec(memory_space=pl.ANY)]...  31.1 us
    pallas_call x1, Pallas kernels, on_device(): pl.pallas_call(functools.partial(update_kernel, PAIR, holders * held_bloc...  19.7 us
    pallas_call x1, Pallas kernels, on_device(): pl.pallas_call(functools.partial(request_kernel, turn, float(members - 1)...  18.4 us
    pallas_call x1, Pallas kernels, on_device(): pl.pallas_call(functools.partial(add_kernel, per), in_specs=[smem, anywhe...  13.7 us

profile of v5, /device:TPU:1, one launch (start us, length us, event | category | flops | bytes accessed | tf_op | source)
XLA Modules:
  0.0 156.1 jit_solution(7335670669054740960)
XLA Ops:
  0.0 0.7 broadcast_divide_fusion
  0.7 0.1 div.39
  0.8 0.7 sign_compare_fusion
  1.5 0.1 ne.117
  1.6 0.1 rem.81
  1.7 0.8 copy.18
  2.4 0.1 reshape.169
  2.5 0.1 broadcast_in_dim.10
  2.6 0.1 reshape.170
  2.7 0.4 convert_reduce_fusion
  3.1 0.3 select_reduce_fusion
  3.4 0.1 convert_element_type.29
  3.5 0.7 pad.4.ask_ref
  4.2 18.4 %requests.1 = (f32[128,1,128]{2,1,0:T(1,128)}, s32[128,1,128]{2,1,0:T(1,128)}, bf16[192,16,128]{2,1,0:T(8,128)(2,1)}) custom-call(bf16[192,128,128]{2,1,0:T(8,128)(2,1)} %anom_ref.3, f32[192,128]{1,0:T(8,128)} %rinv_ref.3, f32[192,128]{1,0:T(8,128)} %innov_ref.1, f32[128,1,128]{2,1,0:T(1,128)} %pad.4.ask_ref), custom_call_target="tpu_custom_call" | custom-call | tf_op jit(solution)/shard_map/requests/pallas_call | solution.py:523
  22.6 0.9 add_multiply_fusion
  23.4 0.7 reshape.178.table_ref
  24.1 66.8 %grams.1 = (bf16[3,8,16,144,128]{4,3,2,1,0:T(8,128)(2,1)}, s32[3,8,8,128]{3,2,1,0:T(8,128)}) custom-call(s32[16384]{0:T(1024)} %bitcast.10, s32[8,128]{1,0:T(8,128)} %reshape.178.table_ref, bf16[192,128,128]{2,1,0:T(8,128)(2,1)} %anom_ref.3, bf16[192,16,128]{2,1,0:T(8,128)(2,1)} %get-tuple-element.12.ext_ref, f32[192,128]{1,0:T(8,128)} %rinv_ref.3, ...), custom_call_target="tpu_custom_call" | custom-call | tf_op jit(solution)/shard_map/grams/pallas_call | solution.py:546
  91.0 13.7 %adds.1.dense_ref = bf16[3,16,384,128]{3,2,1,0:T(8,128)(2,1)} custom-call(s32[24576]{0:T(1024)} %bitcast.12, bf16[3,8,16,144,128]{4,3,2,1,0:T(8,128)(2,1)} %get-tuple-element.14.got_ref), custom_call_target="tpu_custom_call" | custom-call | tf_op jit(solution)/shard_map/adds/pallas_call | solution.py:569
  104.7 0.0 copy-start
  104.7 31.1 %planes.1.acc_ref = f32[16,72,128]{2,1,0:T(8,128)} custom-call(bf16[3,16,384,128]{3,2,1,0:T(8,128)(2,1)} %adds.1.dense_ref), custom_call_target="tpu_custom_call" | custom-call | tf_op jit(solution)/shard_map/planes/pallas_call | solution.py:584
  135.8 0.0 copy-done
  135.8 0.7 copy.21
  136.4 19.7 %update.1 = f32[16,6,128,256]{3,2,1,0:T(8,128)} custom-call(f32[128,1,128]{2,1,0:T(1,128)} %get-tuple-element.10.asked_ref, f32[16,72,128]{2,1,0:T(8,128)} %planes.1.acc_ref, bf16[16,6,128,256]{3,2,1,0:T(8,128)(2,1)} %bitcast.7, f32[16,6,256]{2,1,0:T(8,128)} %bitcast.8), custom_call_target="tpu_custom_call" | custom-call | tf_op jit(solution)/shard_map/update/pallas_call | solution.py:603
  (3 shorter events, 0.0 us)
Async XLA Ops:
  104.7 31.1 %copy-start = (f32[8,2,6,256]{3,1,2,0:T(2,128)S(1)}, f32[8,2,6,256]{3,1,2,0:T(2,128)}, u32[]{:S(2)}) copy-start(f32[8,2,6,256]{3,1,2,0:T(2,128)} %param.10) | copy-start | bytes 294916

commit v6 on v5

--- a/solution.py
+++ b/solution.py
@@ -18,8 +18,8 @@
 BF16 = jnp.bfloat16
 
 
-def request_kernel(turn, members_less, anom_ref, rinv_ref, innov_ref, ask_ref, got_ref, codes_ref, ext_ref, held, row_out, row_in,
-                   sems, send, recv):
+def request_kernel(turn, members_less, anom_ref, rinv_ref, innov_ref, ask_ref, codes_ref, sums_ref, ext_ref, held,
+                   row_in, sems, send, recv):
     blocks, _, width = anom_ref.shape
     turns = blocks // turn
     holders = ask_ref.shape[0]
@@ -36,8 +36,6 @@
         device = (lax.div(other, lat_devices), lax.rem(other, lat_devices))
         return other, device
 
-    for k in range(turns):
-        copy(k).start()
     barrier = pltpu.get_barrier_semaphore()
 
     def signal(step, carry):
@@ -46,9 +44,33 @@
         return carry
 
     lax.fori_loop(1, holders, signal, 0)
-
+    for k in range(turns):
+        copy(k).start()
     innov = innov_ref[...]
+    high = innov.astype(BF16).astype(F32)
+    rest = innov - high
+    mid = rest.astype(BF16).astype(F32)
+    ext = jnp.concatenate(
+        [high[:, None, :], mid[:, None, :], (rest - mid)[:, None, :], jnp.zeros((blocks, 13, width), F32)],
+        axis=1,
+    )
+    ext_ref[...] = ext.astype(BF16)
     first = jnp.sum((rinv_ref[...] * innov * innov).reshape(blocks // 8, 8, width), axis=0)
+    pl.semaphore_wait(barrier, holders - 1)
+
+    def ask(step, carry):
+        other, device = to_holder(step)
+        pltpu.make_async_remote_copy(
+            src_ref=ask_ref.at[other],
+            dst_ref=row_in.at[me],
+            send_sem=send,
+            recv_sem=recv,
+            device_id=device,
+            device_id_type=MESH,
+        ).start()
+        return carry
+
+    lax.fori_loop(1, holders, ask, 0)
 
     def one(k, total):
         copy(k).wait()
@@ -65,39 +87,14 @@
     def whole(x):
         return jnp.sum(jnp.sum(x, axis=0, keepdims=True), axis=1, keepdims=True)
 
-    lane = lax.broadcasted_iota(jnp.int32, (1, width), 1)
-    sums = jnp.where(lane == 6, whole(first), 0.0) + jnp.where(lane == 7, whole(second) / members_less, 0.0)
-    rows = ask_ref[...] + sums[None]
-    row_out[...] = rows
-    high = innov.astype(BF16).astype(F32)
-    rest = innov - high
-    mid = rest.astype(BF16).astype(F32)
-    ext = jnp.concatenate(
-        [high[:, None, :], mid[:, None, :], (rest - mid)[:, None, :], jnp.zeros((blocks, 13, width), F32)],
-        axis=1,
+    lane = lax.broadcasted_iota(jnp.int32, (8, width), 1)
+    sums_ref[...] = jnp.where(
+        lane == 0, whole(first), jnp.where(lane == 1, whole(second) / members_less, 0.0)
     )
-    ext_ref[...] = ext.astype(BF16)
-    pl.semaphore_wait(barrier, holders - 1)
-
-    def ask(step, carry):
-        other, device = to_holder(step)
-        pltpu.make_async_remote_copy(
-            src_ref=row_out.at[other],
-            dst_ref=row_in.at[me],
-            send_sem=send,
-            recv_sem=recv,
-            device_id=device,
-            device_id_type=MESH,
-        ).start()
-        return carry
-
-    lax.fori_loop(1, holders, ask, 0)
-    units_wait(row_out.at[0 : holders - 1], send)
+    units_wait(row_in.at[0 : holders - 1], send)
     units_wait(row_in.at[0 : holders - 1], recv)
-    got_ref[...] = row_in[...]
-    got_ref[me] = row_out[me]
-    codes_ref[...] = row_in[...].astype(jnp.int32)
-    codes_ref[me] = row_out[me].astype(jnp.int32)
+    codes_ref[...] = row_in[...]
+    codes_ref[me] = ask_ref[me]
 
 
 def coordinates():
@@ -153,8 +150,9 @@
     )
 
 
-def gram_kernel(per, lon_patches, lat_patches, code_ref, table_ref, anom_ref, ext_ref, rinv_ref,
-                lon_ref, lat_ref, got_ref, codes_ref, stage, blocks, block_sems, send, recv, own, send2, recv2, own2):
+def gram_kernel(per, lon_patches, lat_patches, code_ref, table_ref, sums_ref, anom_ref, ext_ref, rinv_ref,
+                lon_ref, lat_ref, got_ref, codes_ref, lines_ref, stage, blocks, block_sems, send, recv, own,
+                send2, recv2, own2, send3, recv3, own3):
     me = coordinates()
     xm, ym, zm, cm = me
     mine = (zm, xm, ym)
@@ -189,6 +187,12 @@
                     pltpu.make_async_copy(table_ref, dst, own2.at[q]).start()
                 else:
                     remote(table_ref, dst, send2, recv2, shifted(me, offset)).start()
+                if q == 0:
+                    line = lines_ref.at[source]
+                    if step == 0 and core == 0:
+                        pltpu.make_async_copy(sums_ref, line, own3).start()
+                    else:
+                        remote(sums_ref, line, send3, recv3, shifted(me, offset)).start()
 
     for k in range(chunks):
         fetch(k).wait()
@@ -272,6 +276,9 @@
 
     for q in range(3):
         pltpu.make_async_copy(table_ref, codes_ref.at[q, 0], own2.at[q]).wait()
+    pltpu.make_async_copy(sums_ref, lines_ref.at[0], own3).wait()
+    units_wait(lines_ref.at[0:7], send3)
+    units_wait(lines_ref.at[0:7], recv3)
     units_wait(codes_ref.at[:, 0:7], send2)
     units_wait(codes_ref.at[:, 0:7], recv2)
     units_wait(stage.at[0:16], own)
@@ -336,7 +343,8 @@
         pltpu.make_async_copy(made.at[q], out_ref.at[q], out_sems.at[q]).wait()
 
 
-def plane_kernel(dense_ref, acc_ref, held, mids, lasts, send, recv, send2, recv2, own):
+def plane_kernel(dense_ref, lines_ref, acc_ref, total_ref, held, mids, lasts, sums, parts, send, recv, send2, recv2,
+                 own, send3, recv3):
     me = coordinates()
     xm, ym, zm, _ = me
     firsts, seconds = (xm, ym, zm), (ym, zm, xm)
@@ -346,7 +354,20 @@
     def along(axis, step):
         return shifted(me, tuple(step if a == axis else 0 for a in range(3)) + (0,))
 
+    def give_sums(axis):
+        here = (xm, ym)[axis]
+        for step in (2, 1, 3):
+            remote(sums.at[axis], parts.at[axis, here], send3.at[axis], recv3.at[axis], along(axis, step)).start()
+        parts[axis, here] = sums[axis]
+
+    def take_sums(axis):
+        units_wait(parts.at[axis, 0:3], send3.at[axis])
+        units_wait(parts.at[axis, 0:3], recv3.at[axis])
+        return jnp.sum(parts[axis], axis=0)
+
+    sums[0] = jnp.sum(lines_ref[...], axis=0)
     greet(me, AXIS_PEERS)
+    give_sums(0)
     for q in range(3):
         mine = dense_ref.at[q, pl.ds(firsts[q] * 4, 4)]
         pltpu.make_async_copy(mine, held.at[q, firsts[q]], own.at[q]).start()
@@ -358,6 +379,8 @@
                 along(q, step),
             ).start()
     for q in range(3):
+        if q == 1:
+            sums[1] = take_sums(0)
         pltpu.make_async_copy(dense_ref.at[q, 0:4], held.at[q, 0], own.at[q]).wait()
         units_wait(held.at[q, 0:3], recv.at[q])
 
@@ -379,6 +402,7 @@
                 mids.at[q, other], lasts.at[q, seconds[q]], send2, recv2.at[q], along((q + 1) % 3, step)
             ).start()
         lasts[q, seconds[q]] = mids[q, seconds[q]]
+    give_sums(1)
     for q in range(3):
         units_wait(lasts.at[q, 0:3], recv2.at[q])
 
@@ -392,6 +416,7 @@
             return carry
 
         lax.fori_loop(0, acc_ref.shape[0] // 2, two, 0)
+    total_ref[...] = take_sums(1)
     units_wait(held.at[:, 0:3], send)
     units_wait(lasts.at[:, 0:3], send2)
 
@@ -417,7 +442,7 @@
     return found
 
 
-def update_kernel(count, observations, asked_ref, acc_ref, pert_ref, mean_ref, out_ref, perts, made, sems, out_sems):
+def update_kernel(count, observations, totals_ref, acc_ref, pert_ref, mean_ref, out_ref, perts, made, sems, out_sems):
     patches, fields, members, _ = pert_ref.shape
 
     def take(p):
@@ -428,7 +453,7 @@
 
     for p in range(patches):
         take(p).start()
-    base = float(members - 1) / base_of(asked_ref, observations)
+    base = float(members - 1) / inflation_of(totals_ref, observations)
 
     def one(g, carry):
         update_patches(g * count, count, fields, members, base, acc_ref, mean_ref, perts, made, take, put)
@@ -439,12 +464,8 @@
         put(p).wait()
 
 
-def base_of(asked_ref, observations):
-    total = jnp.sum(asked_ref[...], axis=0)
-    lane = lax.broadcasted_iota(jnp.int32, total.shape, 1)
-    first = jnp.sum(jnp.where(lane == 6, total, 0.0), axis=1, keepdims=True)
-    second = jnp.sum(jnp.where(lane == 7, total, 0.0), axis=1, keepdims=True)
-    return first / (second + float(observations))
+def inflation_of(totals_ref, observations):
+    return totals_ref[0:1, 0:1] / (totals_ref[0:1, 1:2] + float(observations))
 
 
 def update_patches(first, count, fields, members, base, acc_ref, mean_ref, perts, made, take, put):
@@ -518,21 +539,20 @@
     rank = jnp.sum(earlier.astype(jnp.int32), axis=1)
     bucket = holder * per + rank
     requests = jnp.sum(jnp.where(bucket[:, None] == slot[None, :], code[:, None], 0), axis=0)
-    message = jnp.pad(requests.reshape(holders, 1, per).astype(F32), ((0, 0), (0, 0), (0, block_obs - per)))
+    message = jnp.pad(requests.reshape(holders, 1, per), ((0, 0), (0, 0), (0, block_obs - per)))
     turn = 16
-    asked, codes, ext = pl.pallas_call(
+    codes, sums, ext = pl.pallas_call(
         functools.partial(request_kernel, turn, float(members - 1)),
         in_specs=[anywhere, vmem, vmem, vmem],
         out_specs=[vmem, vmem, vmem],
         out_shape=[
-            jax.ShapeDtypeStruct((holders, 1, block_obs), F32),
             jax.ShapeDtypeStruct((holders, 1, block_obs), jnp.int32),
+            jax.ShapeDtypeStruct((8, block_obs), F32),
             jax.ShapeDtypeStruct((held_blocks, 16, block_obs), BF16),
         ],
         scratch_shapes=[
             pltpu.VMEM((held_blocks, members, block_obs), BF16),
-            pltpu.VMEM((holders, 1, block_obs), F32),
-            pltpu.VMEM((holders, 1, block_obs), F32),
+            pltpu.VMEM((holders, 1, block_obs), jnp.int32),
             pltpu.SemaphoreType.DMA((held_blocks // turn,)),
             pltpu.SemaphoreType.DMA,
             pltpu.SemaphoreType.DMA,
@@ -543,13 +563,14 @@
     third = (half + 8) // 3
     short = codes.reshape(holders, block_obs)[:, :8].reshape(holders * 8)
     starts = (((short >> 4) & 7) * lat_patches + ((short >> 7) & 1)) * third
-    got, tables = pl.pallas_call(
+    got, tables, lines = pl.pallas_call(
         functools.partial(gram_kernel, per, lon_patches, lat_patches),
-        in_specs=[smem, anywhere, anywhere, vmem, vmem, vmem, vmem],
-        out_specs=[pl.BlockSpec(memory_space=pl.ANY)] * 2,
+        in_specs=[smem, anywhere, anywhere, anywhere, vmem, vmem, vmem, vmem],
+        out_specs=[anywhere] * 3,
         out_shape=[
             jax.ShapeDtypeStruct((3, 8, 16, per * third, members), BF16),
             jax.ShapeDtypeStruct((3, 8, 8, 128), jnp.int32),
+            jax.ShapeDtypeStruct((8, 8, block_obs), F32),
         ],
         scratch_shapes=[
             pltpu.VMEM((holders, 3, per * third, members), BF16),
@@ -561,10 +582,13 @@
             pltpu.SemaphoreType.DMA,
             pltpu.SemaphoreType.DMA,
             pltpu.SemaphoreType.DMA((3,)),
+            pltpu.SemaphoreType.DMA,
+            pltpu.SemaphoreType.DMA,
+            pltpu.SemaphoreType.DMA,
         ],
         compiler_params=pltpu.CompilerParams(collective_id=0, has_side_effects=True),
         name="grams",
-    )(codes.reshape(holders * block_obs), starts.reshape(8, 128), obs_anom, ext, obs_rinv, obs_lon, obs_lat)
+    )(codes.reshape(holders * block_obs), starts.reshape(8, 128), sums, obs_anom, ext, obs_rinv, obs_lon, obs_lat)
 
     dense = pl.pallas_call(
         functools.partial(add_kernel, per),
@@ -581,24 +605,31 @@
         name="adds",
     )(tables.reshape(3 * 8 * 1024), got)
 
-    acc = pl.pallas_call(
+    acc, totals = pl.pallas_call(
         plane_kernel,
-        in_specs=[pl.BlockSpec(memory_space=pl.ANY)],
-        out_specs=pl.BlockSpec(memory_space=pltpu.VMEM),
-        out_shape=jax.ShapeDtypeStruct((patches, half + 8, members), F32),
+        in_specs=[anywhere, vmem],
+        out_specs=[vmem, vmem],
+        out_shape=[
+            jax.ShapeDtypeStruct((patches, half + 8, members), F32),
+            jax.ShapeDtypeStruct((8, block_obs), F32),
+        ],
         scratch_shapes=[
             pltpu.VMEM((3, 4, 4, patches * third, members), BF16),
             pltpu.VMEM((3, 4, patches * third, members), BF16),
             pltpu.VMEM((3, 4, patches * third, members), BF16),
+            pltpu.VMEM((2, 8, block_obs), F32),
+            pltpu.VMEM((2, 4, 8, block_obs), F32),
             pltpu.SemaphoreType.DMA,
             pltpu.SemaphoreType.DMA((3,)),
             pltpu.SemaphoreType.DMA,
             pltpu.SemaphoreType.DMA((3,)),
             pltpu.SemaphoreType.DMA((3,)),
+            pltpu.SemaphoreType.DMA((2,)),
+            pltpu.SemaphoreType.DMA((2,)),
         ],
         compiler_params=pltpu.CompilerParams(collective_id=1, has_side_effects=True),
         name="planes",
-    )(dense)
+    )(dense, lines)
 
     updated = pl.pallas_call(
         functools.partial(update_kernel, PAIR, holders * held_blocks * block_obs),
@@ -613,7 +644,7 @@
         ],
         name="update",
     )(
-        asked,
+        totals,
         acc,
         state_pert.reshape(patches, fields, members, columns),
         state_mean.reshape(patches, fields, columns),

time: 157 us -> 157 us (level)
  no operation moved by 1% of the time
where the time goes in v6:
time: 157 us
  Pallas kernels  150 us (96%)
  local copies, waits for them, and re-layouts  3.4 us (2%)
  other arithmetic  2.98 us (2%)
    pallas_call x1, Pallas kernels, on_device(): pl.pallas_call(functools.partial(gram_kernel, per, lon_patches, lat_patch...  66.9 us
    pallas_call x1, Pallas kernels, on_device(): pl.pallas_call(plane_kernel, in_specs=[anywhere, vmem], out_specs=[vmem,...  31.9 us
    pallas_call x1, Pallas kernels, on_device(): pl.pallas_call(functools.partial(update_kernel, PAIR, holders * held_bloc...  19.7 us
    pallas_call x1, Pallas kernels, on_device(): pl.pallas_call(functools.partial(request_kernel, turn, float(members - 1)...  18.1 us
    pallas_call x1, Pallas kernels, on_device(): pl.pallas_call(functools.partial(add_kernel, per), in_specs=[smem, anywhe...  13.7 us

profile of v6, /device:TPU:1, one launch (start us, length us, event | category | flops | bytes accessed | tf_op | source)
XLA Modules:
  0.0 156.7 jit_solution(2520669315634490100)
XLA Ops:
  0.0 0.7 broadcast_divide_fusion
  0.7 0.1 div.39
  0.8 0.1 rem.81
  0.9 0.8 copy.18
  1.6 0.1 reshape.158
  1.7 0.1 broadcast_in_dim.10
  1.8 0.1 reshape.159
  1.9 0.7 sign_compare_fusion
  2.6 0.1 ne.117
  2.7 0.4 convert_reduce_fusion
  3.1 0.3 select_reduce_fusion
  3.4 0.1 reshape.160
  3.5 0.7 pad.4.ask_ref
  4.2 18.1 %requests.1 = (s32[128,1,128]{2,1,0:T(1,128)}, f32[8,128]{1,0:T(8,128)}, bf16[192,16,128]{2,1,0:T(8,128)(2,1)}) custom-call(bf16[192,128,128]{2,1,0:T(8,128)(2,1)} %anom_ref.3, f32[192,128]{1,0:T(8,128)} %rinv_ref.3, f32[192,128]{1,0:T(8,128)} %innov_ref.1, s32[128,1,128]{2,1,0:T(1,128)} %pad.4.ask_ref), custom_call_target="tpu_custom_call" | custom-call | tf_op jit(solution)/shard_map/requests/pallas_call | solution.py:544
  22.3 0.9 add_multiply_fusion
  23.2 0.7 reshape.168.table_ref
  23.9 66.9 %grams.1 = (bf16[3,8,16,144,128]{4,3,2,1,0:T(8,128)(2,1)}, s32[3,8,8,128]{3,2,1,0:T(8,128)}, f32[8,8,128]{2,1,0:T(8,128)}) custom-call(s32[16384]{0:T(1024)} %bitcast.10, s32[8,128]{1,0:T(8,128)} %reshape.168.table_ref, f32[8,128]{1,0:T(8,128)} %get-tuple-element.14.sums_ref, bf16[192,128,128]{2,1,0:T(8,128)(2,1)} %anom_ref.3, ...), custom_call_target="tpu_custom_call" | custom-call | tf_op jit(solution)/shard_map/grams/pallas_call | solution.py:566
  90.7 13.7 %adds.1.dense_ref = bf16[3,16,384,128]{3,2,1,0:T(8,128)(2,1)} custom-call(s32[24576]{0:T(1024)} %bitcast.12, bf16[3,8,16,144,128]{4,3,2,1,0:T(8,128)(2,1)} %get-tuple-element.17.got_ref), custom_call_target="tpu_custom_call" | custom-call | tf_op jit(solution)/shard_map/adds/pallas_call | solution.py:593
  104.4 0.0 copy-start
  104.5 31.9 %planes.1 = (f32[16,72,128]{2,1,0:T(8,128)}, f32[8,128]{1,0:T(8,128)}) custom-call(bf16[3,16,384,128]{3,2,1,0:T(8,128)(2,1)} %adds.1.dense_ref, f32[8,8,128]{2,1,0:T(8,128)} %get-tuple-element.18.lines_ref), custom_call_target="tpu_custom_call" | custom-call | tf_op jit(solution)/shard_map/planes/pallas_call | solution.py:608
  136.4 0.0 copy-done
  136.4 0.7 copy.21
  137.1 19.7 %update.1 = f32[16,6,128,256]{3,2,1,0:T(8,128)} custom-call(f32[8,128]{1,0:T(8,128)} %get-tuple-element.19.totals_ref, f32[16,72,128]{2,1,0:T(8,128)} %get-tuple-element.20.acc_ref, bf16[16,6,128,256]{3,2,1,0:T(8,128)(2,1)} %bitcast.7, f32[16,6,256]{2,1,0:T(8,128)} %bitcast.8), custom_call_target="tpu_custom_call" | custom-call | tf_op jit(solution)/shard_map/update/pallas_call | solution.py:634
  (2 shorter events, 0.0 us)
Async XLA Ops:
  104.4 31.9 %copy-start = (f32[8,2,6,256]{3,1,2,0:T(2,128)S(1)}, f32[8,2,6,256]{3,1,2,0:T(2,128)}, u32[]{:S(2)}) copy-start(f32[8,2,6,256]{3,1,2,0:T(2,128)} %param.10) | copy-start | bytes 294916

commit v7 on v6

--- a/solution.py
+++ b/solution.py
@@ -19,58 +19,48 @@
 
 
 def request_kernel(turn, members_less, anom_ref, rinv_ref, innov_ref, ask_ref, codes_ref, sums_ref, ext_ref, held,
-                   row_in, sems, send, recv):
+                   mid, row_in, sems, send, recv, send2, recv2):
     blocks, _, width = anom_ref.shape
     turns = blocks // turn
-    holders = ask_ref.shape[0]
-    lat_devices = lax.axis_size("lat")
-    me = lax.axis_index("lon") * lat_devices + lax.axis_index("lat")
+    lats, lons = ask_ref.shape[0:2]
+    lon, lat = lax.axis_index("lon"), lax.axis_index("lat")
 
     def copy(k):
         return pltpu.make_async_copy(
             anom_ref.at[pl.ds(k * turn, turn)], held.at[pl.ds(k * turn, turn)], sems.at[k]
         )
 
-    def to_holder(step):
-        other = lax.rem(me + step, holders)
-        device = (lax.div(other, lat_devices), lax.rem(other, lat_devices))
-        return other, device
-
     barrier = pltpu.get_barrier_semaphore()
-
-    def signal(step, carry):
-        _, device = to_holder(step)
+    on_lat = [lax.rem(lat + step, lats) for step in range(1, lats)]
+    on_lon = [lax.rem(lon + step, lons) for step in range(1, lons)]
+    for device in [(lon, other) for other in on_lat] + [(other, lat) for other in on_lon]:
         pl.semaphore_signal(barrier, inc=1, device_id=device, device_id_type=MESH)
-        return carry
-
-    lax.fori_loop(1, holders, signal, 0)
     for k in range(turns):
         copy(k).start()
+    mid[lat] = ask_ref[lat]
+    pl.semaphore_wait(barrier, lats + lons - 2)
+
+    def send_rows(src, dst, sent, got, device):
+        pltpu.make_async_remote_copy(
+            src_ref=src, dst_ref=dst, send_sem=sent, recv_sem=got, device_id=device, device_id_type=MESH
+        ).start()
+
+    for other in on_lat:
+        send_rows(ask_ref.at[other], mid.at[lat], send, recv, (lon, other))
     innov = innov_ref[...]
     high = innov.astype(BF16).astype(F32)
     rest = innov - high
-    mid = rest.astype(BF16).astype(F32)
+    middle = rest.astype(BF16).astype(F32)
     ext = jnp.concatenate(
-        [high[:, None, :], mid[:, None, :], (rest - mid)[:, None, :], jnp.zeros((blocks, 13, width), F32)],
+        [high[:, None, :], middle[:, None, :], (rest - middle)[:, None, :], jnp.zeros((blocks, 13, width), F32)],
         axis=1,
     )
     ext_ref[...] = ext.astype(BF16)
     first = jnp.sum((rinv_ref[...] * innov * innov).reshape(blocks // 8, 8, width), axis=0)
-    pl.semaphore_wait(barrier, holders - 1)
-
-    def ask(step, carry):
-        other, device = to_holder(step)
-        pltpu.make_async_remote_copy(
-            src_ref=ask_ref.at[other],
-            dst_ref=row_in.at[me],
-            send_sem=send,
-            recv_sem=recv,
-            device_id=device,
-            device_id_type=MESH,
-        ).start()
-        return carry
-
-    lax.fori_loop(1, holders, ask, 0)
+    units_wait(mid.at[0 : lats - 1], recv)
+    for other in on_lon:
+        send_rows(mid.at[:, other], row_in.at[lon], send2, recv2, (other, lat))
+    row_in[lon] = mid[:, lon]
 
     def one(k, total):
         copy(k).wait()
@@ -91,10 +81,10 @@
     sums_ref[...] = jnp.where(
         lane == 0, whole(first), jnp.where(lane == 1, whole(second) / members_less, 0.0)
     )
-    units_wait(row_in.at[0 : holders - 1], send)
-    units_wait(row_in.at[0 : holders - 1], recv)
+    units_wait(mid.at[0 : lats - 1], send)
+    units_wait(row_in.at[0 : lons - 1], send2)
+    units_wait(row_in.at[0 : lons - 1], recv2)
     codes_ref[...] = row_in[...]
-    codes_ref[me] = ask_ref[me]
 
 
 def coordinates():
@@ -539,21 +529,27 @@
     rank = jnp.sum(earlier.astype(jnp.int32), axis=1)
     bucket = holder * per + rank
     requests = jnp.sum(jnp.where(bucket[:, None] == slot[None, :], code[:, None], 0), axis=0)
-    message = jnp.pad(requests.reshape(holders, 1, per), ((0, 0), (0, 0), (0, block_obs - per)))
+    lons, lats = lax.axis_size("lon"), lax.axis_size("lat")
+    message = jnp.pad(
+        requests.reshape(lons, lats, 1, per).swapaxes(0, 1), ((0, 0), (0, 0), (0, 0), (0, block_obs - per))
+    )
     turn = 16
     codes, sums, ext = pl.pallas_call(
         functools.partial(request_kernel, turn, float(members - 1)),
         in_specs=[anywhere, vmem, vmem, vmem],
         out_specs=[vmem, vmem, vmem],
         out_shape=[
-            jax.ShapeDtypeStruct((holders, 1, block_obs), jnp.int32),
+            jax.ShapeDtypeStruct((lons, lats, 1, block_obs), jnp.int32),
             jax.ShapeDtypeStruct((8, block_obs), F32),
             jax.ShapeDtypeStruct((held_blocks, 16, block_obs), BF16),
         ],
         scratch_shapes=[
             pltpu.VMEM((held_blocks, members, block_obs), BF16),
-            pltpu.VMEM((holders, 1, block_obs), jnp.int32),
+            pltpu.VMEM((lats, lons, 1, block_obs), jnp.int32),
+            pltpu.VMEM((lons, lats, 1, block_obs), jnp.int32),
             pltpu.SemaphoreType.DMA((held_blocks // turn,)),
+            pltpu.SemaphoreType.DMA,
+            pltpu.SemaphoreType.DMA,
             pltpu.SemaphoreType.DMA,
             pltpu.SemaphoreType.DMA,
         ],

time: 157 us -> 157 us (level)
  no operation moved by 1% of the time
where the time goes in v7:
time: 157 us
  Pallas kernels  150 us (96%)
  local copies, waits for them, and re-layouts  4.47 us (3%)
  other arithmetic  2.13 us (1%)
    pallas_call x1, Pallas kernels, on_device(): pl.pallas_call(functools.partial(gram_kernel, per, lon_patches, lat_patch...  67 us
    pallas_call x1, Pallas kernels, on_device(): pl.pallas_call(plane_kernel, in_specs=[anywhere, vmem], out_specs=[vmem,...  31.5 us
    pallas_call x1, Pallas kernels, on_device(): pl.pallas_call(functools.partial(update_kernel, PAIR, holders * held_bloc...  19.7 us
    pallas_call x1, Pallas kernels, on_device(): pl.pallas_call(functools.partial(request_kernel, turn, float(members - 1)...  18.4 us
    pallas_call x1, Pallas kernels, on_device(): pl.pallas_call(functools.partial(add_kernel, per), in_specs=[smem, anywhe...  13.7 us

profile of v7, /device:TPU:1, one launch (start us, length us, event | category | flops | bytes accessed | tf_op | source)
XLA Modules:
  0.0 156.9 jit_solution(1789249367448237557)
XLA Ops:
  0.0 0.7 broadcast_divide_fusion
  0.7 0.1 div.39
  0.8 0.1 rem.81
  0.9 0.8 copy.18
  1.6 0.1 reshape.158
  1.7 0.1 broadcast_in_dim.10
  1.8 0.1 reshape.159
  1.9 0.7 sign_compare_fusion
  2.6 0.1 ne.117
  2.7 0.4 convert_reduce_fusion
  3.1 0.3 select_reduce_fusion
  3.4 0.1 reshape.160
  3.5 0.1 copy.25
  3.6 0.7 pad.4.ask_ref
  4.3 18.4 %requests.1 = (s32[8,16,1,128]{3,2,1,0:T(1,128)}, f32[8,128]{1,0:T(8,128)}, bf16[192,16,128]{2,1,0:T(8,128)(2,1)}) custom-call(bf16[192,128,128]{2,1,0:T(8,128)(2,1)} %anom_ref.3, f32[192,128]{1,0:T(8,128)} %rinv_ref.3, f32[192,128]{1,0:T(8,128)} %innov_ref.1, s32[16,8,1,128]{3,2,1,0:T(1,128)} %pad.4.ask_ref), custom_call_target="tpu_custom_call" | custom-call | tf_op jit(solution)/shard_map/requests/pallas_call | solution.py:537
  22.7 0.9 copy.23
  23.6 0.1 copy.21
  23.7 0.7 reshape.168.table_ref
  24.4 67.0 %grams.1 = (bf16[3,8,16,144,128]{4,3,2,1,0:T(8,128)(2,1)}, s32[3,8,8,128]{3,2,1,0:T(8,128)}, f32[8,8,128]{2,1,0:T(8,128)}) custom-call(s32[16384]{0:T(1024)} %bitcast.13, s32[8,128]{1,0:T(8,128)} %reshape.168.table_ref, f32[8,128]{1,0:T(8,128)} %get-tuple-element.14.sums_ref, bf16[192,128,128]{2,1,0:T(8,128)(2,1)} %anom_ref.3, ...), custom_call_target="tpu_custom_call" | custom-call | tf_op jit(solution)/shard_map/grams/pallas_call | solution.py:562
  91.4 13.7 %adds.1.dense_ref = bf16[3,16,384,128]{3,2,1,0:T(8,128)(2,1)} custom-call(s32[24576]{0:T(1024)} %bitcast.15, bf16[3,8,16,144,128]{4,3,2,1,0:T(8,128)(2,1)} %get-tuple-element.17.got_ref), custom_call_target="tpu_custom_call" | custom-call | tf_op jit(solution)/shard_map/adds/pallas_call | solution.py:589
  105.1 0.0 copy-start
  105.1 31.5 %planes.1 = (f32[16,72,128]{2,1,0:T(8,128)}, f32[8,128]{1,0:T(8,128)}) custom-call(bf16[3,16,384,128]{3,2,1,0:T(8,128)(2,1)} %adds.1.dense_ref, f32[8,8,128]{2,1,0:T(8,128)} %get-tuple-element.18.lines_ref), custom_call_target="tpu_custom_call" | custom-call | tf_op jit(solution)/shard_map/planes/pallas_call | solution.py:604
  136.6 0.0 copy-done
  136.6 0.7 copy.22
  137.3 19.7 %update.1 = f32[16,6,128,256]{3,2,1,0:T(8,128)} custom-call(f32[8,128]{1,0:T(8,128)} %get-tuple-element.19.totals_ref, f32[16,72,128]{2,1,0:T(8,128)} %get-tuple-element.20.acc_ref, bf16[16,6,128,256]{3,2,1,0:T(8,128)(2,1)} %bitcast.10, f32[16,6,256]{2,1,0:T(8,128)} %bitcast.11), custom_call_target="tpu_custom_call" | custom-call | tf_op jit(solution)/shard_map/update/pallas_call | solution.py:630
  (3 shorter events, 0.0 us)
Async XLA Ops:
  105.1 31.5 %copy-start = (f32[8,2,6,256]{3,1,2,0:T(2,128)S(1)}, f32[8,2,6,256]{3,1,2,0:T(2,128)}, u32[]{:S(2)}) copy-start(f32[8,2,6,256]{3,1,2,0:T(2,128)} %param.10) | copy-start | bytes 294916
